TPU v7x, 256 devices: a whole 4x4x8 slice. The times are simulated.
256 devices in a mesh: dp: 64 (over z_lo, x, y), rep: 4 (over z_hi, core).
Axes of the slice: x: 4, y: 4, z: 8 (z_hi: 2, z_lo: 4; z = z_hi * 4 + z_lo), core: 2. Of those that a mesh axis runs over, the one named last changes fastest.
Arguments:
- encoder_out: bfloat16 [1024, 32, 512], P(('dp', 'rep')), may hold values from -6 to 6
- predictor_out: bfloat16 [1024, 17, 512], P(('dp', 'rep')), may hold values from -6 to 6
- w_encoder: bfloat16 [512, 512], replicated, may hold values from -0.25 to 0.25
- w_predictor: bfloat16 [512, 512], replicated, may hold values from -0.25 to 0.25
- w_joint: bfloat16 [512, 500], replicated, may hold values from -1.296875 to 1.296875
- joint_bias: float32 [500], replicated, may hold values from -8 to 150
- labels: int32 [1024, 16], P(('dp', 'rep')), may hold values from 1 to 499
- frame_lens: int32 [1024], P(('dp', 'rep')), may hold values from 16 to 32, as said below
- label_lens: int32 [1024], P(('dp', 'rep')), may hold values from 1 to 16, as said below
- prune_starts: int32 [1024, 32], P(('dp', 'rep')), may hold values from 0 to 12, as said below
Outputs:
- grad_encoder: float32 [512, 512], replicated
- grad_predictor: float32 [512, 512], replicated
- grad_joint: float32 [512, 500], replicated
- grad_bias: float32 [500], replicated
- loss_mean: float32 [], replicated
Inputs may be any that keep to these rules, and one draw needn't show every extreme that they name: `frame_lens`: utterance 0 has 32 frames. `label_lens`: utterance 1 has 16 labels. prune_starts[b,0] = 0; from frame frame_lens[b]-1 on, the start equals max(label_lens[b] - 4, 0), and no start exceeds that value; the starts of consecutive frames differ by at most 3.
All inputs are finite; a program needn't handle non-finite values.
Results may differ from a plain program's by a relative error of at most 0.0059.
Values sent between devices are 32-bit elements; how exact they have to be, the bound alone decides.
No kernel may reach another device: no remote copies, remote signals or barrier semaphores. Data moves between devices by JAX's collectives and lax.ppermute only.
A program may use at most 64 MiB of HBM per device.

v0:
```python
import jax
import jax.numpy as jnp
from jax import lax
from jax.sharding import PartitionSpec as P

S = 5


NEG_FILL = -10000.0


def together(arrays, axis):
    ends = [0]
    for a in arrays:
        ends.append(ends[-1] + a.size)
    total = lax.psum(jnp.concatenate([a.ravel() for a in arrays]), axis)
    return tuple((total[b:e].reshape(a.shape) for a, b, e in zip(arrays, ends, ends[1:])))


def cut_along(value, dim, length):
    shape = value.shape
    blocks = value.reshape(*shape[:dim], length, shape[dim] // length, *shape[dim + 1 :])
    return jnp.moveaxis(blocks, dim, 0)


def sum_at_owner(value, axis, dim):
    blocks = cut_along(value, dim, lax.axis_size(axis))
    arrived = lax.all_to_all(blocks, axis, split_axis=0, concat_axis=0, tiled=True)
    return arrived.sum(axis=0)


def sent_together(arrays, axis, dim, along):
    ends, at = ([], 0)
    for a in arrays[:-1]:
        at += a.shape[along]
        ends.append(at)
    both = jnp.concatenate(arrays, axis=along)
    return tuple(jnp.split(sum_at_owner(both, axis, dim), ends, axis=along))


def sent_together_2(arrays, axis, dim, along):
    both = jnp.concatenate(arrays, axis=along)
    filled, at, done = (lax.all_gather(both, axis, axis=dim, tiled=True), 0, [])
    for a in arrays:
        done.append(lax.slice_in_dim(filled, at, at + a.shape[along], axis=along))
        at += a.shape[along]
    return tuple(done)


def within_frame(entering, emission_now):
    columns = [entering[:, 0]]
    for offset in range(1, entering.shape[1]):
        columns.append(
            jnp.logaddexp(entering[:, offset], columns[-1] + emission_now[:, offset - 1])
        )
    return jnp.stack(columns, axis=1)


def lattice(blank_lp, emission, prune_starts, frame_lens, label_lens):
    batches, frames, band = blank_lp.shape
    offsets = jnp.arange(band, dtype=jnp.int32)
    opening = jnp.where(offsets == 0, 0.0, NEG_FILL).astype(blank_lp.dtype)
    forward = within_frame(jnp.broadcast_to(opening, (batches, band)), emission[:, 0])
    shifts = prune_starts[:, 1:] - prune_starts[:, :-1]

    def advance(forward, inputs):
        frame_index, blank_prev, shift_now, emission_now = inputs
        source = offsets[None, :] + shift_now[:, None]
        inside = (source >= 0) & (source < band)
        picked = jnp.take_along_axis(forward + blank_prev, jnp.clip(source, 0, band - 1), axis=1)
        entering = jnp.where(inside, picked, NEG_FILL)
        updated = within_frame(entering, emission_now)
        return (jnp.where((frame_index < frame_lens)[:, None], updated, forward), None)

    inputs = (
        jnp.arange(1, frames, dtype=jnp.int32),
        jnp.swapaxes(blank_lp[:, :-1], 0, 1),
        jnp.swapaxes(shifts, 0, 1),
        jnp.swapaxes(emission[:, 1:], 0, 1),
    )
    forward, _ = lax.scan(advance, forward, inputs)
    last_frame = frame_lens - 1
    last_start = jnp.take_along_axis(prune_starts, last_frame[:, None], axis=1)[:, 0]
    final_pos = label_lens - last_start
    end_row = jnp.take_along_axis(blank_lp, last_frame[:, None, None], axis=1)[:, 0]
    end_blank = jnp.take_along_axis(end_row, final_pos[:, None], axis=1)[:, 0]
    end_forward = jnp.take_along_axis(forward, final_pos[:, None], axis=1)[:, 0]
    return end_forward + end_blank


def frame_loss(logits, labels, prune_starts, frame_lens, label_lens):
    batches, frames, band, vocab = logits.shape
    positions = prune_starts[:, :, None] + jnp.arange(band, dtype=jnp.int32)
    log_probs = jax.nn.log_softmax(logits, axis=-1)
    label_slots = labels.shape[1]
    next_label = jnp.take_along_axis(
        labels, jnp.minimum(positions, label_slots - 1).reshape(batches, -1), axis=1
    )
    next_label = next_label.reshape(positions.shape)
    emission = jnp.take_along_axis(log_probs, next_label[..., None], axis=-1)[..., 0]
    emission = jnp.where(positions < label_lens[:, None, None], emission, NEG_FILL)
    blank_lp = jnp.where(positions <= label_lens[:, None, None], log_probs[..., 0], NEG_FILL)
    likelihood = lattice(blank_lp, emission, prune_starts, frame_lens, label_lens)
    return jnp.sum(-likelihood / frame_lens.astype(jnp.float32))


def shards(
    encoder_out,
    predictor_out,
    w_encoder,
    w_predictor,
    w_joint,
    joint_bias,
    labels,
    frame_lens,
    label_lens,
    prune_starts,
):
    batches, frames, enc_width = encoder_out.shape
    row_count, pred_width = (predictor_out.shape[1], predictor_out.shape[2])
    joint_width = w_encoder.shape[1]
    vocab = w_joint.shape[1]
    enc_proj = jnp.dot(
        encoder_out.reshape(-1, enc_width), w_encoder, preferred_element_type=jnp.float32
    )
    enc_proj = enc_proj.astype(jnp.bfloat16).reshape(batches, frames, joint_width)
    pred_proj = jnp.dot(
        predictor_out.reshape(-1, pred_width), w_predictor, preferred_element_type=jnp.float32
    )
    pred_proj = pred_proj.astype(jnp.bfloat16).reshape(batches, row_count, joint_width)
    positions = prune_starts[:, :, None] + jnp.arange(S, dtype=jnp.int32)
    flat_pos = positions.reshape(batches, frames * S)
    picked = jnp.take_along_axis(pred_proj, flat_pos[:, :, None], axis=1).reshape(
        batches, frames, S, joint_width
    )
    active = jnp.tanh(enc_proj[:, :, None, :].astype(jnp.float32) + picked.astype(jnp.float32))
    active_flat = active.reshape(-1, joint_width)
    hidden = active_flat.astype(jnp.bfloat16)
    logits = (jnp.dot(hidden, w_joint, preferred_element_type=jnp.float32) + joint_bias).reshape(
        batches, frames, S, vocab
    )
    loss_sum, pullback = jax.vjp(
        lambda scores: frame_loss(scores, labels, prune_starts, frame_lens, label_lens), logits
    )
    (grad_logits,) = pullback(jnp.ones((), jnp.float32))
    grad_flat = grad_logits.reshape(-1, vocab)
    grad_low = grad_flat.astype(jnp.bfloat16)
    grad_joint = lax.dot_general(
        hidden, grad_low, (((0,), (0,)), ((), ())), preferred_element_type=jnp.float32
    )
    grad_bias = jnp.sum(grad_flat, axis=0)
    grad_joint, grad_bias, loss_sum = together((grad_joint, grad_bias, loss_sum), ("dp", "rep"))
    grad_hidden = lax.dot_general(
        grad_low, w_joint, (((1,), (1,)), ((), ())), preferred_element_type=jnp.float32
    )
    grad_pre = (grad_hidden * (1.0 - active_flat * active_flat)).reshape(
        batches, frames, S, joint_width
    )
    grad_enc_proj = jnp.sum(grad_pre, axis=2).astype(jnp.bfloat16).reshape(-1, joint_width)
    grad_pre_low = grad_pre.astype(jnp.bfloat16).reshape(batches, frames * S, joint_width)
    placing = (flat_pos[:, :, None] == jnp.arange(row_count, dtype=jnp.int32)).astype(jnp.bfloat16)
    grad_pred_proj = jnp.einsum(
        "bnu,bnj->buj", placing, grad_pre_low, preferred_element_type=jnp.float32
    ).astype(jnp.bfloat16)
    grad_encoder = lax.dot_general(
        encoder_out.reshape(-1, enc_width),
        grad_enc_proj,
        (((0,), (0,)), ((), ())),
        preferred_element_type=jnp.float32,
    )
    grad_predictor = lax.dot_general(
        predictor_out.reshape(-1, pred_width),
        grad_pred_proj.reshape(-1, joint_width),
        (((0,), (0,)), ((), ())),
        preferred_element_type=jnp.float32,
    )
    shares = sent_together((grad_encoder, grad_predictor), "dp", 0, 1)
    shares = together((shares[0], shares[1]), "rep")
    grad_encoder, grad_predictor = sent_together_2((shares[0], shares[1]), "dp", 0, 1)
    utterances = batches * lax.axis_size("dp") * lax.axis_size("rep")
    return (grad_encoder, grad_predictor, grad_joint, grad_bias, loss_sum / utterances)


def solution(mesh):
    in_specs = (
        P(("dp", "rep"), None, None),
        P(("dp", "rep"), None, None),
        P(),
        P(),
        P(),
        P(),
        P(("dp", "rep"), None),
        P(("dp", "rep")),
        P(("dp", "rep")),
        P(("dp", "rep"), None),
    )
    out_specs = (P(), P(), P(), P(), P())
    return jax.shard_map(shards, mesh=mesh, in_specs=in_specs, out_specs=out_specs, check_vma=False)
```

profile of v0, /device:TPU:8, one launch (start us, length us, event | category | flops | bytes accessed | tf_op | source)
XLA Modules:
  0.0 743.3 jit_solution(17639605489156758142)
XLA Ops:
  15.9 7.4 gather_fusion.2
  23.3 2.0 fusion.119
  26.4 5.6 gather_fusion.1
  35.2 2.4 fusion.60
  37.6 7.7 %gather_fusion.3 = f32[640]{0:T(1024)S(1)} fusion(f32[4,32,5,500]{3,1,2,0:T(8,128)S(1)} %fusion.60, s32[640]{0:T(1024)S(1)} %reshape.1750), kind=kCustom, calls=%fused_computation.5 | custom fusion | bytes 15360 | tf_op jit(solution)/shard_map/jvp(jit(take_along_axis))/gather | solution.py:100
  47.3 3.3 add_select_fusion.6
  51.2 112.7 %while.54 = (s32[]{:T(128)}, f32[4,5]{1,0:T(4,128)S(1)}, s32[31,4,5,1]{2,1,3,0:T(4,128)S(1)}, pred[31,4,5]{2,1,0:T(4,128)(4,1)S(1)}, f32[31,4]{1,0:T(8,128)S(1)}...) while((s32[]{:T(128)}, f32[4,5]{1,0:T(4,128)S(1)}, ...), condition=%wide.region_3.4_spmd.clone.clone, body=%wide.region_2.3_spmd.clone.clone.sunk | while | flops 1146 | bytes 9505 | solution.py:81
  167.5 111.0 %while.53 = (s32[]{:T(128)}, f32[4,5]{1,0:T(4,128)S(1)}, f32[31,4,5]{2,0,1:T(8,128)S(1)}, f32[31,4,5]{2,1,0:T(4,128)S(1)}, pred[31,4,5]{2,1,0:T(4,128)(4,1)S(1)}...) while((s32[]{:T(128)}, f32[4,5]{1,0:T(4,128)S(1)}, ...), condition=%wide.region_6.8_spmd, body=%wide.region_4.7_spmd.sunk | while | flops 483 | bytes 13185 | solution.py:81
  169.0 2.0 scatter_fusion
  172.6 2.0 scatter_fusion
  176.2 2.0 scatter_fusion
  179.8 2.0 scatter_fusion
  183.3 2.0 scatter_fusion
  186.9 2.0 scatter_fusion
  190.5 2.0 scatter_fusion
  194.1 2.0 scatter_fusion
  197.7 2.0 scatter_fusion
  201.2 2.0 scatter_fusion
  204.8 2.0 scatter_fusion
  208.4 2.0 scatter_fusion
  212.0 2.0 scatter_fusion
  215.5 2.0 scatter_fusion
  219.1 2.0 scatter_fusion
  222.7 2.0 scatter_fusion
  226.3 2.0 scatter_fusion
  229.9 2.0 scatter_fusion
  233.4 2.0 scatter_fusion
  237.0 2.0 scatter_fusion
  240.6 2.0 scatter_fusion
  244.2 2.0 scatter_fusion
  251.3 2.0 scatter_fusion
  254.9 2.0 scatter_fusion
  262.1 2.0 scatter_fusion
  265.7 2.0 scatter_fusion
  269.2 2.0 scatter_fusion
  276.4 2.0 scatter_fusion
  285.6 2.9 fusion.120
  288.4 2.6 reshape.1705
  291.1 2.3 reduce_sum.66
  295.2 2.8 pad_maximum_fusion
  298.0 2.9 copy.317
  300.9 12.2 %all-to-all-start = ((f32[64,8,1024]{2,1,0:T(8,128)}), f32[64,8,1024]{2,1,0:T(8,128)}, u32[]{:S(2)}, u32[]{:S(2)}) async-start(f32[64,8,1024]{2,1,0:T(8,128)} %bitcast.302), calls=%async_computation | async-start | bytes 4194304 | tf_op jit(solution)/shard_map/all_to_all | solution.py:28
  316.8 7.7 %concatenate.15 = f32[256501]{0:T(1024)} concatenate(f32[256000]{0:T(1024)S(1)} %reshape.1709, f32[500]{0:T(512)S(1)} %copy-done.15, f32[1]{0:T(128)} %bitcast.54), dimensions={0} | concatenate | bytes 2052008 | tf_op jit(solution)/shard_map/concatenate | solution.py:16
  324.7 39.8 %all-to-all-done = f32[64,8,1024]{2,1,0:T(8,128)} async-done(((f32[64,8,1024]{2,1,0:T(8,128)}), f32[64,8,1024]{2,1,0:T(8,128)}, u32[]{:S(2)}, u32[]{:S(2)}) %all-to-all-start) | async-done | bytes 2097184 | tf_op jit(solution)/shard_map/all_to_all | solution.py:28
  366.2 20.6 %psum.14 = f32[8192]{0:T(1024)S(1)} all-reduce(f32[8192]{0:T(1024)S(1)} %pad_maximum_fusion.1), channel_id=1, replica_groups=mesh['dp'=64,'rep'=4] {'rep'}, use_global_device_ids=true, to_apply=%region_11.13 | all-reduce | flops 8192 | bytes 65536 | tf_op jit(solution)/shard_map/psum | solution.py:16
  387.5 197.9 %all-reduce.19.cloned.1.call-done = f32[256501]{0:T(1024)} async-done(((f32[256501]{0:T(1024)}), f32[256501]{0:T(1024)}) %all-reduce.19.cloned.1.call-update) | async-done | bytes 1026020 | tf_op jit(solution)/shard_map/psum | solution.py:16
  590.8 140.9 %all-gather.2.cloned.1.call-done = f32[512,1024]{1,0:T(8,128)} async-done(((f32[8,1024]{1,0:T(8,128)}), f32[512,1024]{1,0:T(8,128)}) %all-gather.2.cloned.1.call-update) | async-done | bytes 2097168 | tf_op jit(solution)/shard_map/all_gather | solution.py:43
  731.7 3.0 fusion.116
  (1816 shorter events, 201.2 us)
Async XLA Ops:
  8.0 3.8 copy-start
  8.0 3.8 copy-start.13
  12.0 0.7 copy-start.10
  15.9 7.4 copy-start.4
  15.9 7.4 copy-start.17
  25.8 0.7 copy-start.1
  26.4 6.1 copy-start.2
  37.6 8.3 %copy-start.16 = (s32[4]{0:T(128)S(1)}, s32[4]{0:T(128)}, u32[]{:S(2)}) copy-start(s32[4]{0:T(128)} %param.24) | copy-start | bytes 52
  37.6 9.6 %copy-start.18 = (s32[4]{0:T(128)S(1)}, s32[4]{0:T(128)}, u32[]{:S(2)}) copy-start(s32[4]{0:T(128)} %param.23) | copy-start | bytes 52
  167.5 113.7 %copy-start.3 = (f32[4,32,5,500]{3,2,1,0:T(8,128)S(1)}, f32[4,32,5,500]{3,2,1,0:T(8,128)}, u32[]{:S(2)}) copy-start(f32[4,32,5,500]{3,2,1,0:T(8,128)} %reshape.1702) | copy-start | bytes 3840004
  283.0 0.8 copy-start.8
  283.9 1.7 copy-start.5
  283.9 1.7 copy-start.6
  291.1 2.3 copy-start.14
  291.1 3.6 copy-start.12
  300.9 63.5 %all-to-all-start = ((f32[64,8,1024]{2,1,0:T(8,128)}), f32[64,8,1024]{2,1,0:T(8,128)}, u32[]{:S(2)}, u32[]{:S(2)}) async-start(f32[64,8,1024]{2,1,0:T(8,128)} %bitcast.302), calls=%async_computation | async-start | bytes 4194304 | tf_op jit(solution)/shard_map/all_to_all | solution.py:28
  313.1 0.9 copy-start.11
  313.1 272.3 %all-reduce.19.cloned.1.call-start = ((), (), s32[]{:S(2)}) async-start(), calls=%async_computation.2 | async-start | bytes 2056192 | tf_op jit(solution)/shard_map/psum | solution.py:16
  314.0 1.1 copy-start.9
  315.8 1.1 copy-start.15
  324.6 407.1 %all-gather.2.cloned.1.call-start = ((), (), s32[]{:S(2)}) async-start(), calls=%async_computation.1 | async-start | bytes 2129920 | tf_op jit(solution)/shard_map/all_gather | solution.py:43
  585.5 1.2 slice-start
  587.6 1.3 copy-start.7
Sparse Core Ops, SparseCore 0:
  324.7 260.6 all-reduce.18
Sparse Core Ops, SparseCore 1:
  387.6 344.0 all-gather.1
where the time goes:
time: 744 us; the launch traced here: 743 us
  waiting for transfers between devices  379 us (51%)
  local copies, waits for them, and re-layouts  159 us (21%)
  other arithmetic  143 us (19%)
  blocking collectives  20.6 us (3%)
  between operations  17.9 us (2%)
  starting transfers between devices  12.3 us (2%)
  matrix products  8.87 us (1%)
    psum x1, waiting for transfers between devices, together(): total = lax.psum(jnp.concatenate([a.ravel() for a in arrays]), axis)  198 us
    all_gather x1, waiting for transfers between devices, sent_together_2(): filled, at, done = (lax.all_gather(both, axis, axis=dim, tiled=True), 0, [])  141 us
    scatter-add x62, other arithmetic, advance(): jnp.take_along_axis(forward + blank_prev, jnp.clip(source, 0, band - 1),...  63.1 us
    all_to_all x1, waiting for transfers between devices, sum_at_owner(): lax.all_to_all(blocks, axis, split_axis=0, concat_axis=0, tiled=True)  39.8 us
    gather x93, local copies, waits for them, and re-layouts, advance(): jnp.take_along_axis(forward + blank_prev, jnp.clip(source, 0, band - 1),...  31.4 us
    squeeze x403, local copies, waits for them, and re-layouts, lattice(): forward, _ = lax.scan(advance, forward, inputs)  24.1 us
    psum x1, blocking collectives, together(): total = lax.psum(jnp.concatenate([a.ravel() for a in arrays]), axis)  20.6 us
    lt x31, other arithmetic, advance(): frame_index < frame_lens  20.1 us
  transfers between devices with their start and end apart: 3, of which 3 were waited for; matrix products, arithmetic and copies ran while one was open for 2% of the time, Pallas kernels for 0%

commit v1 on v0

v1 whole, which is shorter than its diff:
```python
import functools

import jax
import jax.numpy as jnp
from jax import lax
from jax.experimental import pallas as pl
from jax.experimental.pallas import tpu as pltpu
from jax.sharding import PartitionSpec as P

S = 5
NEG_FILL = -10000.0
LOW = -1e30
F32 = jnp.float32
BF16 = jnp.bfloat16
AXES = ("zl", "x", "y", "zh", "c")
PAIRS = tuple((j, s) for s in range(S) for j in range(s + 1))


def over_rows(a, b):
    return lax.dot_general(a, b, (((0,), (0,)), ((), ())), preferred_element_type=F32)


def per_utterance(index, values):
    out = jnp.where(index == 0, values[0], values[-1])
    for b in range(1, len(values) - 1):
        out = jnp.where(index == b, values[b], out)
    return out


def shifted(rows, amount, lowest, fill):
    width = len(rows)
    span = {i: rows[i] if 0 <= i < width else fill for i in range(lowest, width + lowest + 7)}
    bits = amount - lowest
    for bit in (4, 2, 1):
        on = (bits & bit) != 0
        top = max(span)
        span = {
            i: jnp.where(on, span[i + bit], span[i])
            for i in span
            if i + bit <= top
        }
    return [span[s + lowest] for s in range(width)]


def joint_kernel(
    frames_ref, lens_ref, enc_ref, pred_ref, w_enc_ref, w_pred_ref, w_joint_ref,
    bias_ref, labels_ref, starts_ref,
    keep_ref, send_ref,
    pred_s, w_joint_s, bias_s, active_s, hidden_s, scores_s, low_s, picks_s,
    blank_s, emit_s, shift_s, terms_s, sums_s, state_s, gblank_s, grad_enc_s, grad_pred_s,
):
    count, row_count, _ = pred_ref.shape
    vocab = w_joint_ref.shape[1]
    slots = labels_ref.shape[1]
    rows = enc_ref.shape[0]
    frames = rows // count
    width = w_joint_s.shape[1]
    stride = pred_s.shape[0] // count

    frame_len = [frames_ref[b] for b in range(count)]
    label_len = [lens_ref[b] for b in range(count)]

    pred_s[...] = jnp.zeros_like(pred_s)
    for b in range(count):
        pred_s[b * stride : b * stride + row_count, :] = pred_ref[b]
    last = (width // 128 - 1) * 128
    w_joint_s[:, last:] = jnp.zeros((w_joint_s.shape[0], 128), BF16)
    w_joint_s[:, :vocab] = w_joint_ref[...]
    bias_s[...] = jnp.full_like(bias_s, LOW)
    bias_s[:, :vocab] = bias_ref[...]

    eye = lax.broadcasted_iota(jnp.int32, (frames, frames), 0) == lax.broadcasted_iota(
        jnp.int32, (frames, frames), 1
    )
    starts_f = starts_ref[...].astype(F32)
    lane_b = lax.broadcasted_iota(jnp.int32, (frames, 128), 1)
    start_cols = []
    start_tb = jnp.zeros((frames, 128), F32)
    for b in range(count):
        line = jnp.broadcast_to(starts_f[b : b + 1, :], (frames, frames))
        col = jnp.sum(jnp.where(eye, line, 0.0), axis=1, keepdims=True)
        start_cols.append(col)
        start_tb = jnp.where(lane_b == b, col, start_tb)
    start_col = jnp.concatenate(start_cols, axis=0).astype(jnp.int32)
    start_tb = start_tb.astype(jnp.int32)
    row_b = lax.broadcasted_iota(jnp.int32, (rows, 1), 0) // frames
    label_len_col = per_utterance(row_b, label_len)
    label_len_row = per_utterance(lax.broadcasted_iota(jnp.int32, (1, 128), 1), label_len)
    frame_len_row = per_utterance(lax.broadcasted_iota(jnp.int32, (1, 128), 1), frame_len)
    shift_s[0:1, :] = jnp.zeros((1, 128), jnp.int32)
    shift_s[1:frames, :] = start_tb[1:, :] - start_tb[:-1, :]

    enc_proj = jnp.dot(enc_ref[...], w_enc_ref[...], preferred_element_type=F32).astype(BF16)
    enc_proj = enc_proj.astype(F32)
    pred_proj = jnp.dot(pred_s[...], w_pred_ref[...], preferred_element_type=F32).astype(BF16)

    lane_u = lax.broadcasted_iota(jnp.int32, (rows, count * stride), 1)
    lane_k = lax.broadcasted_iota(jnp.int32, (rows, slots), 1)
    label_rows = jnp.concatenate(
        [jnp.broadcast_to(labels_ref[b : b + 1, :].astype(F32), (frames, slots)) for b in range(count)],
        axis=0,
    )
    lane_v = lax.broadcasted_iota(jnp.int32, (rows, width), 1)
    next_label, scale = [], []
    for s in range(S):
        pos = start_col + s
        pick = (lane_u == row_b * stride + pos).astype(F32).astype(BF16)
        picks_s[s] = pick
        picked = jnp.dot(pick, pred_proj, preferred_element_type=F32)
        active = jnp.tanh(enc_proj + picked)
        active_s[s] = active
        hidden = active.astype(BF16)
        hidden_s[s * rows : (s + 1) * rows, :] = hidden
        logits = jnp.dot(hidden, w_joint_s[...], preferred_element_type=F32) + bias_s[...]
        peak = jnp.max(logits, axis=1, keepdims=True)
        raised = jnp.exp(logits - peak)
        scores_s[s] = raised
        total = jnp.sum(raised, axis=1, keepdims=True)
        norm = peak + jnp.log(total)
        scale.append(1.0 / total)
        blank = jnp.where(pos <= label_len_col, logits[:, 0:1] - norm, NEG_FILL)
        blank_tb = jnp.zeros((frames, 128), F32)
        for b in range(count):
            blank_tb = jnp.where(lane_b == b, blank[b * frames : (b + 1) * frames, :], blank_tb)
        blank_s[s] = blank_tb
        if s < S - 1:
            label = jnp.sum(
                jnp.where(lane_k == pos, label_rows, 0.0), axis=1, keepdims=True
            ).astype(jnp.int32)
            next_label.append(label)
            emit = jnp.sum(jnp.where(lane_v == label, logits, 0.0), axis=1, keepdims=True)
            emit = jnp.where(pos < label_len_col, emit - norm, NEG_FILL)
            emit_tb = jnp.zeros((frames, 128), F32)
            for b in range(count):
                emit_tb = jnp.where(lane_b == b, emit[b * frames : (b + 1) * frames, :], emit_tb)
            emit_s[s] = emit_tb

    fill = jnp.full((1, 128), NEG_FILL, F32)
    state = None
    for t in range(frames):
        if t == 0:
            entering = [jnp.zeros((1, 128), F32)] + [fill] * (S - 1)
        else:
            leaving = [state[s] + blank_s[s, t - 1 : t, :] for s in range(S)]
            entering = shifted(leaving, shift_s[t : t + 1, :], -3, fill)
        emits = [emit_s[s, t : t + 1, :] for s in range(S - 1)]
        updated = []
        for s in range(S):
            routes = []
            for j in range(s + 1):
                way = entering[j]
                for i in range(j, s):
                    way = way + emits[i]
                routes.append(way)
            best = routes[0]
            for r in routes[1:]:
                best = jnp.maximum(best, r)
            terms = [jnp.exp(r - best) for r in routes]
            total = terms[0]
            for r in terms[1:]:
                total = total + r
            for j in range(s + 1):
                terms_s[PAIRS.index((j, s)), t : t + 1, :] = terms[j]
            sums_s[s, t : t + 1, :] = total
            updated.append(best + jnp.log(total))
        if t == 0:
            state = updated
        else:
            live = t < frame_len_row
            state = [jnp.where(live, n, o) for n, o in zip(updated, state)]

    frame_tb = lax.broadcasted_iota(jnp.int32, (frames, 128), 0)
    ending = frame_tb == frame_len_row - 1
    valid = lax.broadcasted_iota(jnp.int32, (1, 128), 1) < count
    final_start = jnp.sum(jnp.where(ending, start_tb.astype(F32), 0.0), axis=0, keepdims=True)
    final_pos = label_len_row - final_start.astype(jnp.int32)
    share = jnp.where(valid, -1.0 / frame_len_row.astype(F32), 0.0)
    likelihood = jnp.zeros((1, 128), F32)
    grads = []
    for s in range(S):
        here = final_pos == s
        end_blank = jnp.sum(jnp.where(ending, blank_s[s], 0.0), axis=0, keepdims=True)
        likelihood = jnp.where(here, state[s] + end_blank, likelihood)
        grads.append(jnp.where(here, share, 0.0))
        gblank_s[s] = jnp.where(ending & here, share, 0.0)
    loss = jnp.sum(jnp.where(valid, likelihood * share, 0.0), axis=1, keepdims=True)

    for s in range(S):
        inverse = 1.0 / sums_s[s]
        for j in range(s + 1):
            terms_s[PAIRS.index((j, s))] = terms_s[PAIRS.index((j, s))] * inverse

    none = jnp.zeros((1, 128), F32)
    for t in range(frames - 1, 0, -1):
        live = t < frame_len_row
        for s in range(S):
            state_s[s, t : t + 1, :] = jnp.where(live, grads[s], 0.0)
        back = []
        for j in range(S):
            parts = [grads[s] * terms_s[PAIRS.index((j, s)), t : t + 1, :] for s in range(j, S)]
            total = parts[0]
            for r in parts[1:]:
                total = total + r
            back.append(total)
        earlier = shifted(back, -shift_s[t : t + 1, :], -3, none)
        for s in range(S):
            gblank_s[s, t - 1 : t, :] += jnp.where(live, earlier[s], 0.0)
        grads = [jnp.where(live, n, o) for n, o in zip(earlier, grads)]
    for s in range(S):
        state_s[s, 0:1, :] = grads[s]

    def column(table):
        return jnp.concatenate([table[:, b : b + 1] for b in range(count)], axis=0)

    gemit = [jnp.zeros((frames, 128), F32) for _ in range(S - 1)]
    for j, s in PAIRS:
        if j < s:
            flow = state_s[s] * terms_s[PAIRS.index((j, s))]
            for i in range(j, s):
                gemit[i] = gemit[i] + flow
    bias_total = jnp.zeros((1, width), F32)
    for s in range(S):
        pos = start_col + s
        gblank = jnp.where(pos <= label_len_col, column(gblank_s[s]), 0.0)
        if s < S - 1:
            gemit_col = jnp.where(pos < label_len_col, column(gemit[s]), 0.0)
            weight = (gblank + gemit_col) * scale[s]
        else:
            weight = gblank * scale[s]
        grad = jnp.where(lane_v == 0, gblank, 0.0) - scores_s[s] * weight
        if s < S - 1:
            grad = grad + jnp.where(lane_v == next_label[s], gemit_col, 0.0)
        bias_total = bias_total + jnp.sum(grad, axis=0, keepdims=True)
        low_s[s * rows : (s + 1) * rows, :] = grad.astype(BF16)

    bias_col = jnp.transpose(jnp.broadcast_to(bias_total, (8, width)))[:, 0:1]
    row_j = lax.broadcasted_iota(jnp.int32, bias_col.shape, 0)
    side = jnp.where(row_j == width - 1, loss, bias_col)

    grad_enc_proj = jnp.zeros((rows, w_enc_ref.shape[1]), F32)
    grad_pred_proj = jnp.zeros((count * stride, w_pred_ref.shape[1]), F32)
    for s in range(S):
        grad_hidden = lax.dot_general(
            low_s[s * rows : (s + 1) * rows, :], w_joint_s[...], (((1,), (1,)), ((), ())),
            preferred_element_type=F32,
        )
        active = active_s[s]
        grad_pre = grad_hidden * (1.0 - active * active)
        grad_enc_proj = grad_enc_proj + grad_pre
        grad_pred_proj = grad_pred_proj + over_rows(picks_s[s], grad_pre.astype(BF16))
    grad_enc_s[...] = grad_enc_proj.astype(BF16)
    grad_pred_s[...] = grad_pred_proj.astype(BF16)

    core = lax.axis_index("c")
    half = width // 2
    for out_ref, which in ((send_ref, 1 - core), (keep_ref, core)):
        columns = pl.ds(pl.multiple_of(which * half, half), half)
        products = (
            over_rows(enc_ref[...], grad_enc_s[:, columns]),
            over_rows(pred_s[...], grad_pred_s[:, columns]),
            over_rows(hidden_s[...], low_s[:, columns]),
        )
        at = 0
        for m, product in enumerate(products):
            if m == 2:
                lane = lax.broadcasted_iota(jnp.int32, product.shape, 1) + which * half
                product = jnp.where(lane == vocab, side, product)
            for j in range(half // 128):
                out_ref[at : at + width, :] = product[:, j * 128 : (j + 1) * 128]
                at += width


def local_grads(
    encoder_out, predictor_out, w_encoder, w_predictor, w_joint, joint_bias,
    labels, frame_lens, label_lens, prune_starts,
):
    count, frames, enc_width = encoder_out.shape
    pred_width = predictor_out.shape[2]
    joint_width, vocab = w_joint.shape
    rows = count * frames
    width = -(-vocab // 128) * 128
    stride = 32
    vmem = pl.BlockSpec(memory_space=pltpu.VMEM)
    smem = pl.BlockSpec(memory_space=pltpu.SMEM)
    return pl.pallas_call(
        joint_kernel,
        out_shape=(jax.ShapeDtypeStruct((3 * width * width // 256, 128), F32),) * 2,
        in_specs=[smem, smem] + [vmem] * 8,
        out_specs=(vmem, vmem),
        scratch_shapes=[
            pltpu.VMEM((count * stride, pred_width), BF16),
            pltpu.VMEM((joint_width, width), BF16),
            pltpu.VMEM((1, width), F32),
            pltpu.VMEM((S, rows, joint_width), F32),
            pltpu.VMEM((S * rows, joint_width), BF16),
            pltpu.VMEM((S, rows, width), F32),
            pltpu.VMEM((S * rows, width), BF16),
            pltpu.VMEM((S, rows, count * stride), BF16),
            pltpu.VMEM((S, frames, 128), F32),
            pltpu.VMEM((S - 1, frames, 128), F32),
            pltpu.VMEM((frames, 128), jnp.int32),
            pltpu.VMEM((len(PAIRS), frames, 128), F32),
            pltpu.VMEM((S, frames, 128), F32),
            pltpu.VMEM((S, frames, 128), F32),
            pltpu.VMEM((S, frames, 128), F32),
            pltpu.VMEM((rows, joint_width), BF16),
            pltpu.VMEM((count * stride, joint_width), BF16),
        ],
        name="joint",
    )(
        frame_lens, label_lens, encoder_out.reshape(rows, enc_width), predictor_out,
        w_encoder, w_predictor, w_joint, joint_bias.reshape(1, vocab), labels, prune_starts,
    )


def unpack_kernel(utterances, mine_ref, other_ref, enc_ref, pred_ref, joint_ref, bias_ref, loss_ref):
    core = lax.axis_index("c")
    width = enc_ref.shape[0]
    vocab = joint_ref.shape[1]
    half = width // 256

    def place(refs):
        for h in range(2):
            for m, out_ref in enumerate((enc_ref, pred_ref, joint_ref)):
                for j in range(half):
                    at = (m * half + j) * width
                    lane = (h * half + j) * 128
                    size = min(128, out_ref.shape[1] - lane)
                    out_ref[:, lane : lane + size] = refs[h][at : at + width, :size]
        at = (2 * half + (vocab // 128) % half) * width
        tile = refs[vocab // 128 // half][at : at + width, :]
        side = jnp.transpose(tile)[vocab % 128 : vocab % 128 + 1, :]
        bias_ref[...] = side[:, :vocab]
        loss_ref[...] = side[:, width - 1 :] / utterances

    @pl.when(core == 0)
    def _():
        place((mine_ref, other_ref))

    @pl.when(core != 0)
    def _():
        place((other_ref, mine_ref))


def swap_cores(value):
    return lax.ppermute(value, "c", [(0, 1), (1, 0)])


def sum_at_owner(value, axes):
    members = lax.axis_size(axes)
    arrived = lax.all_to_all(value, axes, split_axis=0, concat_axis=0, tiled=True)
    return arrived.reshape(members, -1, value.shape[1]).sum(axis=0)


def from_all(value, axes):
    members = lax.axis_size(axes)
    spread = jnp.broadcast_to(value[None], (members, *value.shape))
    spread = spread.reshape(-1, value.shape[1])
    return lax.all_to_all(spread, axes, split_axis=0, concat_axis=0, tiled=True)


def shards(*args):
    keep, send = local_grads(*args)
    mine = keep + swap_cores(send)
    mine = sum_at_owner(mine, ("x", "y"))
    mine = sum_at_owner(mine, ("zl", "zh"))
    mine = from_all(mine, ("zl", "zh"))
    mine = from_all(mine, ("x", "y"))
    other = swap_cores(mine)
    width, vocab = args[4].shape
    utterances = args[0].shape[0] * lax.axis_size(AXES)
    vmem = pl.BlockSpec(memory_space=pltpu.VMEM)
    grad_encoder, grad_predictor, grad_joint, grad_bias, loss = pl.pallas_call(
        functools.partial(unpack_kernel, utterances),
        out_shape=(
            jax.ShapeDtypeStruct((width, width), F32),
            jax.ShapeDtypeStruct((width, width), F32),
            jax.ShapeDtypeStruct((width, vocab), F32),
            jax.ShapeDtypeStruct((1, vocab), F32),
            jax.ShapeDtypeStruct((1, 1), F32),
        ),
        in_specs=[vmem, vmem],
        out_specs=(vmem,) * 5,
        name="unpack",
    )(mine, other)
    return grad_encoder, grad_predictor, grad_joint, grad_bias.reshape(vocab), loss.reshape(())


def solution(mesh):
    mesh = jax.sharding.Mesh(mesh.devices.reshape(4, 4, 4, 2, 2), AXES)
    in_specs = (
        P(AXES, None, None), P(AXES, None, None), P(), P(), P(), P(),
        P(AXES, None), P(AXES), P(AXES), P(AXES, None),
    )
    return jax.shard_map(
        shards, mesh=mesh, in_specs=in_specs, out_specs=(P(),) * 5, check_vma=False
    )
```

time: 744 us -> 110 us (0.15)
  the two profiles are of different devices: /device:TPU:8 before, /device:TPU:1 now
where the time goes in v1:
time: 110 us
  blocking collectives  71.4 us (65%)
  Pallas kernels  13.2 us (12%)
  starting transfers between devices  9.36 us (9%)
  local copies, waits for them, and re-layouts  7.41 us (7%)
  waiting for transfers between devices  6.28 us (6%)
  other arithmetic  1.66 us (2%)
    all_to_all x2, blocking collectives, sum_at_owner(): lax.all_to_all(value, axes, split_axis=0, concat_axis=0, tiled=True)  41.1 us
    all_to_all x2, blocking collectives, from_all(): return lax.all_to_all(spread, axes, split_axis=0, concat_axis=0, tiled=True)  30.3 us
    ppermute x2, starting transfers between devices, swap_cores(): return lax.ppermute(value, 'c', [(0, 1), (1, 0)])  9.36 us
    pallas_call x1, Pallas kernels, local_grads(): pl.pallas_call(joint_kernel, out_shape=(jax.ShapeDtypeStruct((3 * width *...  9.26 us
    unnamed x7, local copies, waits for them, and re-layouts  7.25 us
    ppermute x2, waiting for transfers between devices, swap_cores(): return lax.ppermute(value, 'c', [(0, 1), (1, 0)])  6.28 us
    pallas_call x1, Pallas kernels, shards(): pl.pallas_call(functools.partial(unpack_kernel, utterances), out_shape=(j...  3.95 us
  transfers between devices with their start and end apart: 2, of which 2 were waited for; matrix products, arithmetic and copies ran while one was open for 0% of the time, Pallas kernels for 0%

profile of v1, /device:TPU:1, one launch (start us, length us, event | category | flops | bytes accessed | tf_op | source)
XLA Modules:
  0.0 110.0 jit_solution(12932742471635556711)
XLA Ops:
  0.6 1.5 %copy.18.pred_ref = bf16[4,17,512]{2,1,0:T(8,128)(2,1)} copy(bf16[4,17,512]{2,0,1:T(4,128)(2,1)} %param.11) | data formatting | bytes 139264 | tf_op args[1]
  2.2 2.0 %copy.19.w_joint_ref = bf16[512,500]{1,0:T(8,128)(2,1)} copy(bf16[512,500]{0,1:T(8,128)(2,1)} %param.14) | data formatting | bytes 1024000 | tf_op args[4]
  4.2 9.3 %joint.1 = (f32[3072,128]{1,0:T(8,128)}, f32[3072,128]{1,0:T(8,128)}) custom-call(s32[4]{0:T(128)} %frames_ref.1, s32[4]{0:T(128)} %lens_ref.1, bf16[128,512]{1,0:T(8,128)(2,1)} %bitcast.13, bf16[4,17,512]{2,1,0:T(8,128)(2,1)} %copy.18.pred_ref, bf16[512,512]{1,0:T(8,128)(2,1)} %w_enc_ref.1, bf16[512,512]{1,0:T(8,128)(2,1)} %w_pred_ref.1, ...), custom_call_target="tpu_custom_call" | custom-call | tf_op jit(solution)/shard_map/joint/pallas_call | solution.py:285
  13.5 3.2 %collective-permute-start = (f32[3072,128]{1,0:T(8,128)}, f32[3072,128]{1,0:T(8,128)S(1)}, u32[]{:S(2)}, u32[]{:S(2)}) collective-permute-start(f32[3072,128]{1,0:T(8,128)} %get-tuple-element.13), channel_id=1, source_target_pairs={{0,1},{1,0},{2,3},{3,2},{4,5},{5,4},{6,7},{7,6},{8,9},{9,8},{10,11... | collective-permute-start | bytes 4718600 | tf_op jit(solution)/shard_map/ppermute | solution.py:346
  16.7 3.2 %collective-permute-done = f32[3072,128]{1,0:T(8,128)S(1)} collective-permute-done((f32[3072,128]{1,0:T(8,128)}, f32[3072,128]{1,0:T(8,128)S(1)}, u32[]{:S(2)}, u32[]{:S(2)}) %collective-permute-start) | collective-permute-done | bytes 1572896 | tf_op jit(solution)/shard_map/ppermute | solution.py:346
  19.9 1.6 %add.3 = f32[3072,128]{1,0:T(8,128)S(1)} add(f32[3072,128]{1,0:T(8,128)} %get-tuple-element.12, f32[3072,128]{1,0:T(8,128)S(1)} %collective-permute-done) | non-fusion elementwise | flops 393216 | bytes 4718592 | tf_op jit(solution)/shard_map/add | solution.py:364
  21.5 26.5 %all_to_all.32 = f32[16,192,128]{2,1,0:T(8,128)S(1)} all-to-all(f32[16,192,128]{2,1,0:T(8,128)S(1)} %bitcast.10), channel_id=1, replica_groups=mesh['zl'=4,'x'=4,'y'=4,'zh'=2,'c'=2] {'x','y'}, dimensions={0} | all-to-all | bytes 3145728 | tf_op jit(solution)/shard_map/all_to_all | solution.py:351
  48.0 0.1 reduce_sum.18
  48.0 14.6 %all_to_all.33 = f32[8,24,128]{2,1,0:T(8,128)S(1)} all-to-all(f32[8,24,128]{2,1,0:T(8,128)S(1)} %bitcast.11), channel_id=1, replica_groups=mesh['zl'=4,'x'=4,'y'=4,'zh'=2,'c'=2] {'zl','zh'}, dimensions={0} | all-to-all | bytes 196608 | tf_op jit(solution)/shard_map/all_to_all | solution.py:351
  62.7 9.2 %all_to_all.34 = f32[8,24,128]{2,1,0:T(8,128)S(1)} all-to-all(f32[8,24,128]{2,1,0:T(8,128)S(1)} %broadcast_in_dim.6), channel_id=1, replica_groups=mesh['zl'=4,'x'=4,'y'=4,'zh'=2,'c'=2] {'zl','zh'}, dimensions={0} | all-to-all | bytes 196608 | tf_op jit(solution)/shard_map/all_to_all | solution.py:359
  71.9 0.1 broadcast_in_dim.16
  72.1 21.0 %all_to_all.35 = f32[16,192,128]{2,1,0:T(8,128)S(1)} all-to-all(f32[16,192,128]{2,1,0:T(8,128)S(1)} %broadcast_in_dim.16), channel_id=1, replica_groups=mesh['zl'=4,'x'=4,'y'=4,'zh'=2,'c'=2] {'x','y'}, dimensions={0} | all-to-all | bytes 3145728 | tf_op jit(solution)/shard_map/all_to_all | solution.py:359
  93.1 0.0 copy-start
  93.1 6.2 %collective-permute-start.1 = (f32[3072,128]{1,0:T(8,128)S(1)}, f32[3072,128]{1,0:T(8,128)S(1)}, u32[]{:S(2)}, u32[]{:S(2)}) collective-permute-start(f32[3072,128]{1,0:T(8,128)S(1)} %bitcast.8), channel_id=1, source_target_pairs={{0,1},{1,0},{2,3},{3,2},{4,5},{5,4},{6,7},{7,6},{8,9},{9,8},{10,11... | collective-permute-start | bytes 4718600 | tf_op jit(solution)/shard_map/ppermute | solution.py:346
  99.3 3.0 %collective-permute-done.1.other_ref = f32[3072,128]{1,0:T(8,128)S(1)} collective-permute-done((f32[3072,128]{1,0:T(8,128)S(1)}, f32[3072,128]{1,0:T(8,128)S(1)}, u32[]{:S(2)}, u32[]{:S(2)}) %collective-permute-start.1) | collective-permute-done | bytes 1572896 | tf_op jit(solution)/shard_map/ppermute | solution.py:346
  102.3 0.0 copy-done
  102.3 0.0 copy-start.1
  102.3 1.2 %copy-done.1 = f32[3072,128]{1,0:T(8,128)} copy-done((f32[3072,128]{1,0:T(8,128)}, f32[3072,128]{1,0:T(8,128)S(1)}, u32[]{:S(2)}) %copy-start.1) | copy-done | bytes 1572888
  103.5 4.0 %unpack.1 = (f32[512,512]{1,0:T(8,128)}, f32[512,512]{1,0:T(8,128)}, f32[512,500]{1,0:T(8,128)}, f32[1,500]{1,0:T(1,128)}, f32[1,1]{1,0:T(1,128)}) custom-call(f32[3072,128]{1,0:T(8,128)} %bitcast.9, f32[3072,128]{1,0:T(8,128)} %copy-done.1), custom_call_target="tpu_custom_call" | custom-call | tf_op jit(solution)/shard_map/unpack/pallas_call | solution.py:373
  107.5 2.5 %copy.20 = f32[512,500]{0,1:T(8,128)} copy(f32[512,500]{1,0:T(8,128)} %get-tuple-element.26) | data formatting | bytes 2048000
  (2 shorter events, 0.0 us)
Async XLA Ops:
  13.5 6.4 %collective-permute-start = (f32[3072,128]{1,0:T(8,128)}, f32[3072,128]{1,0:T(8,128)S(1)}, u32[]{:S(2)}, u32[]{:S(2)}) collective-permute-start(f32[3072,128]{1,0:T(8,128)} %get-tuple-element.13), channel_id=1, source_target_pairs={{0,1},{1,0},{2,3},{3,2},{4,5},{5,4},{6,7},{7,6},{8,9},{9,8},{10,11... | collective-permute-start | bytes 4718600 | tf_op jit(solution)/shard_map/ppermute | solution.py:346
  93.1 9.2 %copy-start = (f32[16,192,128]{2,1,0:T(8,128)}, f32[16,192,128]{2,1,0:T(8,128)S(1)}, u32[]{:S(2)}) copy-start(f32[16,192,128]{2,1,0:T(8,128)S(1)} %all_to_all.35) | copy-start | bytes 4718596
  93.1 9.2 %collective-permute-start.1 = (f32[3072,128]{1,0:T(8,128)S(1)}, f32[3072,128]{1,0:T(8,128)S(1)}, u32[]{:S(2)}, u32[]{:S(2)}) collective-permute-start(f32[3072,128]{1,0:T(8,128)S(1)} %bitcast.8), channel_id=1, source_target_pairs={{0,1},{1,0},{2,3},{3,2},{4,5},{5,4},{6,7},{7,6},{8,9},{9,8},{10,11... | collective-permute-start | bytes 4718600 | tf_op jit(solution)/shard_map/ppermute | solution.py:346
  102.3 1.2 %copy-start.1 = (f32[3072,128]{1,0:T(8,128)}, f32[3072,128]{1,0:T(8,128)S(1)}, u32[]{:S(2)}) copy-start(f32[3072,128]{1,0:T(8,128)S(1)} %collective-permute-done.1.other_ref) | copy-start | bytes 4718596

commit v2 on v1

--- a/solution.py
+++ b/solution.py
@@ -12,7 +12,9 @@
 LOW = -1e30
 F32 = jnp.float32
 BF16 = jnp.bfloat16
-AXES = ("zl", "x", "y", "zh", "c")
+AXES = ("zq", "zp", "x", "y", "zh", "c")
+NEAR = ("zp", "x", "y")
+FAR = ("zq", "zh")
 PAIRS = tuple((j, s) for s in range(S) for j in range(s + 1))
 
 
@@ -43,31 +45,48 @@
 
 
 def joint_kernel(
+    frames_hbm, lens_hbm, enc_hbm, pred_hbm, w_enc_hbm, w_pred_hbm, w_joint_hbm,
+    bias_hbm, labels_hbm, starts_hbm,
+    keep_ref, send_ref,
     frames_ref, lens_ref, enc_ref, pred_ref, w_enc_ref, w_pred_ref, w_joint_ref,
-    bias_ref, labels_ref, starts_ref,
-    keep_ref, send_ref,
+    bias_ref, labels_ref, starts_ref, load_sems,
     pred_s, w_joint_s, bias_s, active_s, hidden_s, scores_s, low_s, picks_s,
     blank_s, emit_s, shift_s, terms_s, sums_s, state_s, gblank_s, grad_enc_s, grad_pred_s,
 ):
-    count, row_count, _ = pred_ref.shape
-    vocab = w_joint_ref.shape[1]
+    loads = {
+        name: pltpu.make_async_copy(src, dst, load_sems.at[i])
+        for i, (name, src, dst) in enumerate((
+            ("starts", starts_hbm, starts_ref),
+            ("frames", frames_hbm, frames_ref),
+            ("lens", lens_hbm, lens_ref),
+            ("enc", enc_hbm, enc_ref),
+            ("w_enc", w_enc_hbm, w_enc_ref),
+            ("pred", pred_hbm, pred_ref),
+            ("w_pred", w_pred_hbm, w_pred_ref),
+            ("labels", labels_hbm, labels_ref),
+            ("bias", bias_hbm, bias_ref),
+            ("w_joint", w_joint_hbm, w_joint_ref),
+        ))
+    }
+    for load in loads.values():
+        load.start()
+
+    row_count, count, _ = pred_ref.shape
+    vocab = w_joint_ref.shape[0]
     slots = labels_ref.shape[1]
     rows = enc_ref.shape[0]
     frames = rows // count
-    width = w_joint_s.shape[1]
-    stride = pred_s.shape[0] // count
-
+    width = w_joint_s.shape[0]
+    places = pred_s.shape[0]
+
+    pred_s[...] = jnp.zeros_like(pred_s)
+    last = (width // 128 - 1) * 128
+    w_joint_s[last:, :] = jnp.zeros((128, w_joint_s.shape[1]), BF16)
+    bias_s[...] = jnp.full_like(bias_s, LOW)
+    for name in ("starts", "frames", "lens"):
+        loads[name].wait()
     frame_len = [frames_ref[b] for b in range(count)]
     label_len = [lens_ref[b] for b in range(count)]
-
-    pred_s[...] = jnp.zeros_like(pred_s)
-    for b in range(count):
-        pred_s[b * stride : b * stride + row_count, :] = pred_ref[b]
-    last = (width // 128 - 1) * 128
-    w_joint_s[:, last:] = jnp.zeros((w_joint_s.shape[0], 128), BF16)
-    w_joint_s[:, :vocab] = w_joint_ref[...]
-    bias_s[...] = jnp.full_like(bias_s, LOW)
-    bias_s[:, :vocab] = bias_ref[...]
 
     eye = lax.broadcasted_iota(jnp.int32, (frames, frames), 0) == lax.broadcasted_iota(
         jnp.int32, (frames, frames), 1
@@ -90,11 +109,19 @@
     shift_s[0:1, :] = jnp.zeros((1, 128), jnp.int32)
     shift_s[1:frames, :] = start_tb[1:, :] - start_tb[:-1, :]
 
+    for name in ("enc", "w_enc", "pred", "w_pred"):
+        loads[name].wait()
+    for u in range(row_count):
+        pred_s[u * count : (u + 1) * count, :] = pred_ref[u]
     enc_proj = jnp.dot(enc_ref[...], w_enc_ref[...], preferred_element_type=F32).astype(BF16)
     enc_proj = enc_proj.astype(F32)
     pred_proj = jnp.dot(pred_s[...], w_pred_ref[...], preferred_element_type=F32).astype(BF16)
 
-    lane_u = lax.broadcasted_iota(jnp.int32, (rows, count * stride), 1)
+    for name in ("labels", "bias", "w_joint"):
+        loads[name].wait()
+    w_joint_s[:vocab, :] = w_joint_ref[...]
+    bias_s[:, :vocab] = bias_ref[...]
+    lane_u = lax.broadcasted_iota(jnp.int32, (rows, places), 1)
     lane_k = lax.broadcasted_iota(jnp.int32, (rows, slots), 1)
     label_rows = jnp.concatenate(
         [jnp.broadcast_to(labels_ref[b : b + 1, :].astype(F32), (frames, slots)) for b in range(count)],
@@ -104,14 +131,17 @@
     next_label, scale = [], []
     for s in range(S):
         pos = start_col + s
-        pick = (lane_u == row_b * stride + pos).astype(F32).astype(BF16)
+        pick = (lane_u == pos * count + row_b).astype(F32).astype(BF16)
         picks_s[s] = pick
         picked = jnp.dot(pick, pred_proj, preferred_element_type=F32)
         active = jnp.tanh(enc_proj + picked)
         active_s[s] = active
         hidden = active.astype(BF16)
         hidden_s[s * rows : (s + 1) * rows, :] = hidden
-        logits = jnp.dot(hidden, w_joint_s[...], preferred_element_type=F32) + bias_s[...]
+        logits = lax.dot_general(
+            hidden, w_joint_s[...], (((1,), (1,)), ((), ())), preferred_element_type=F32
+        )
+        logits = logits + bias_s[...]
         peak = jnp.max(logits, axis=1, keepdims=True)
         raised = jnp.exp(logits - peak)
         scores_s[s] = raised
@@ -233,21 +263,17 @@
         bias_total = bias_total + jnp.sum(grad, axis=0, keepdims=True)
         low_s[s * rows : (s + 1) * rows, :] = grad.astype(BF16)
 
-    bias_col = jnp.transpose(jnp.broadcast_to(bias_total, (8, width)))[:, 0:1]
-    row_j = lax.broadcasted_iota(jnp.int32, bias_col.shape, 0)
-    side = jnp.where(row_j == width - 1, loss, bias_col)
-
     grad_enc_proj = jnp.zeros((rows, w_enc_ref.shape[1]), F32)
-    grad_pred_proj = jnp.zeros((count * stride, w_pred_ref.shape[1]), F32)
-    for s in range(S):
-        grad_hidden = lax.dot_general(
-            low_s[s * rows : (s + 1) * rows, :], w_joint_s[...], (((1,), (1,)), ((), ())),
-            preferred_element_type=F32,
+    grad_pred_proj = jnp.zeros((places, w_pred_ref.shape[1]), F32)
+    for s in range(S):
+        grad_hidden = jnp.dot(
+            low_s[s * rows : (s + 1) * rows, :], w_joint_s[...], preferred_element_type=F32
         )
         active = active_s[s]
         grad_pre = grad_hidden * (1.0 - active * active)
         grad_enc_proj = grad_enc_proj + grad_pre
         grad_pred_proj = grad_pred_proj + over_rows(picks_s[s], grad_pre.astype(BF16))
+    bias_s[...] = bias_total
     grad_enc_s[...] = grad_enc_proj.astype(BF16)
     grad_pred_s[...] = grad_pred_proj.astype(BF16)
 
@@ -258,16 +284,18 @@
         products = (
             over_rows(enc_ref[...], grad_enc_s[:, columns]),
             over_rows(pred_s[...], grad_pred_s[:, columns]),
-            over_rows(hidden_s[...], low_s[:, columns]),
+            over_rows(low_s[...], hidden_s[:, columns]),
         )
         at = 0
-        for m, product in enumerate(products):
-            if m == 2:
-                lane = lax.broadcasted_iota(jnp.int32, product.shape, 1) + which * half
-                product = jnp.where(lane == vocab, side, product)
+        for product in products:
             for j in range(half // 128):
                 out_ref[at : at + width, :] = product[:, j * 128 : (j + 1) * 128]
                 at += width
+        base = at - (half // 128) * width + vocab
+        for j in range(half // 128):
+            lanes = pl.ds(pl.multiple_of(which * half + j * 128, 128), 128)
+            out_ref[base + j * width : base + j * width + 1, :] = bias_s[:, lanes]
+            out_ref[base + j * width + 1 : base + j * width + 2, :] = jnp.broadcast_to(loss, (1, 128))
 
 
 def local_grads(
@@ -279,23 +307,33 @@
     joint_width, vocab = w_joint.shape
     rows = count * frames
     width = -(-vocab // 128) * 128
-    stride = 32
+    places = 128
     vmem = pl.BlockSpec(memory_space=pltpu.VMEM)
-    smem = pl.BlockSpec(memory_space=pltpu.SMEM)
     return pl.pallas_call(
         joint_kernel,
-        out_shape=(jax.ShapeDtypeStruct((3 * width * width // 256, 128), F32),) * 2,
-        in_specs=[smem, smem] + [vmem] * 8,
+        out_shape=(pltpu.VMEM((3 * width * width // 256, 128), F32),) * 2,
+        in_specs=[pl.BlockSpec(memory_space=pltpu.HBM)] * 10,
         out_specs=(vmem, vmem),
         scratch_shapes=[
-            pltpu.VMEM((count * stride, pred_width), BF16),
-            pltpu.VMEM((joint_width, width), BF16),
+            pltpu.SMEM((count,), jnp.int32),
+            pltpu.SMEM((count,), jnp.int32),
+            pltpu.VMEM((rows, enc_width), BF16),
+            pltpu.VMEM((predictor_out.shape[1], count, pred_width), BF16),
+            pltpu.VMEM(w_encoder.shape, BF16),
+            pltpu.VMEM(w_predictor.shape, BF16),
+            pltpu.VMEM((vocab, joint_width), BF16),
+            pltpu.VMEM((1, vocab), F32),
+            pltpu.VMEM(labels.shape, jnp.int32),
+            pltpu.VMEM(prune_starts.shape, jnp.int32),
+            pltpu.SemaphoreType.DMA((10,)),
+            pltpu.VMEM((places, pred_width), BF16),
+            pltpu.VMEM((width, joint_width), BF16),
             pltpu.VMEM((1, width), F32),
             pltpu.VMEM((S, rows, joint_width), F32),
             pltpu.VMEM((S * rows, joint_width), BF16),
             pltpu.VMEM((S, rows, width), F32),
             pltpu.VMEM((S * rows, width), BF16),
-            pltpu.VMEM((S, rows, count * stride), BF16),
+            pltpu.VMEM((S, rows, places), BF16),
             pltpu.VMEM((S, frames, 128), F32),
             pltpu.VMEM((S - 1, frames, 128), F32),
             pltpu.VMEM((frames, 128), jnp.int32),
@@ -304,19 +342,20 @@
             pltpu.VMEM((S, frames, 128), F32),
             pltpu.VMEM((S, frames, 128), F32),
             pltpu.VMEM((rows, joint_width), BF16),
-            pltpu.VMEM((count * stride, joint_width), BF16),
+            pltpu.VMEM((places, joint_width), BF16),
         ],
+        compiler_params=pltpu.CompilerParams(vmem_limit_bytes=56 * 2**20),
         name="joint",
     )(
-        frame_lens, label_lens, encoder_out.reshape(rows, enc_width), predictor_out,
-        w_encoder, w_predictor, w_joint, joint_bias.reshape(1, vocab), labels, prune_starts,
+        frame_lens, label_lens, encoder_out.reshape(rows, enc_width),
+        jnp.swapaxes(predictor_out, 0, 1),        w_encoder, w_predictor, w_joint.T, joint_bias.reshape(1, vocab), labels, prune_starts,
     )
 
 
 def unpack_kernel(utterances, mine_ref, other_ref, enc_ref, pred_ref, joint_ref, bias_ref, loss_ref):
     core = lax.axis_index("c")
     width = enc_ref.shape[0]
-    vocab = joint_ref.shape[1]
+    vocab = joint_ref.shape[0]
     half = width // 256
 
     def place(refs):
@@ -325,13 +364,15 @@
                 for j in range(half):
                     at = (m * half + j) * width
                     lane = (h * half + j) * 128
-                    size = min(128, out_ref.shape[1] - lane)
-                    out_ref[:, lane : lane + size] = refs[h][at : at + width, :size]
-        at = (2 * half + (vocab // 128) % half) * width
-        tile = refs[vocab // 128 // half][at : at + width, :]
-        side = jnp.transpose(tile)[vocab % 128 : vocab % 128 + 1, :]
-        bias_ref[...] = side[:, :vocab]
-        loss_ref[...] = side[:, width - 1 :] / utterances
+                    size = out_ref.shape[0]
+                    out_ref[:, lane : lane + 128] = refs[h][at : at + size, :]
+            for j in range(half):
+                at = (2 * half + j) * width + vocab
+                lane = (h * half + j) * 128
+                size = min(128, vocab - lane)
+                bias_ref[:, lane : lane + size] = refs[h][at : at + 1, :size]
+        at = 2 * half * width + vocab + 1
+        loss_ref[...] = refs[0][at : at + 1, 0:1] / utterances
 
     @pl.when(core == 0)
     def _():
@@ -359,13 +400,25 @@
     return lax.all_to_all(spread, axes, split_axis=0, concat_axis=0, tiled=True)
 
 
+def sum_everywhere(value, axes):
+    sizes = [lax.axis_size(a) for a in axes]
+    assert sizes == [2, 2]
+    arrived = []
+    for step in (2, 1, 3):
+        pairs = [
+            (2 * (n % 2) + n // 2, 2 * ((n + step) % 4 % 2) + (n + step) % 4 // 2)
+            for n in range(4)
+        ]
+        arrived.append(lax.ppermute(value, axes, pairs))
+    return (value + arrived[0]) + (arrived[1] + arrived[2])
+
+
 def shards(*args):
     keep, send = local_grads(*args)
     mine = keep + swap_cores(send)
-    mine = sum_at_owner(mine, ("x", "y"))
-    mine = sum_at_owner(mine, ("zl", "zh"))
-    mine = from_all(mine, ("zl", "zh"))
-    mine = from_all(mine, ("x", "y"))
+    mine = sum_at_owner(mine, NEAR)
+    mine = sum_everywhere(mine, FAR)
+    mine = from_all(mine, NEAR)
     other = swap_cores(mine)
     width, vocab = args[4].shape
     utterances = args[0].shape[0] * lax.axis_size(AXES)
@@ -375,19 +428,20 @@
         out_shape=(
             jax.ShapeDtypeStruct((width, width), F32),
             jax.ShapeDtypeStruct((width, width), F32),
-            jax.ShapeDtypeStruct((width, vocab), F32),
+            jax.ShapeDtypeStruct((vocab, width), F32),
             jax.ShapeDtypeStruct((1, vocab), F32),
             jax.ShapeDtypeStruct((1, 1), F32),
         ),
         in_specs=[vmem, vmem],
         out_specs=(vmem,) * 5,
+        compiler_params=pltpu.CompilerParams(vmem_limit_bytes=20 * 2**20),
         name="unpack",
     )(mine, other)
-    return grad_encoder, grad_predictor, grad_joint, grad_bias.reshape(vocab), loss.reshape(())
+    return grad_encoder, grad_predictor, grad_joint.T, grad_bias.reshape(vocab), loss.reshape(())
 
 
 def solution(mesh):
-    mesh = jax.sharding.Mesh(mesh.devices.reshape(4, 4, 4, 2, 2), AXES)
+    mesh = jax.sharding.Mesh(mesh.devices.reshape(2, 2, 4, 4, 2, 2), AXES)
     in_specs = (
         P(AXES, None, None), P(AXES, None, None), P(), P(), P(), P(),
         P(AXES, None), P(AXES), P(AXES), P(AXES, None),

time: 110 us -> 88.5 us (0.80)
  blocking collectives: 71.4 us -> 52.1 us
  local copies, waits for them, and re-layouts: 7.41 us -> 0.17 us
  starting transfers between devices: 9.36 us -> 15.8 us
  Pallas kernels: 13.2 us -> 9.51 us
  waiting for transfers between devices: 6.28 us -> 9.81 us
  other arithmetic: 1.66 us -> 0.26 us
    all_to_all x2 -> x1, blocking collectives: 41.1 us -> 27.8 us  [sum_at_owner(): lax.all_to_all(value, axes, split_axis=0, concat_axis=0, tiled=True)]
    ppermute x0 -> x3, starting transfers between devices: none -> 8.45 us  [sum_everywhere(): arrived.append(lax.ppermute(value, axes, pairs))]
    unnamed x7 -> x0, local copies, waits for them, and re-layouts: 7.25 us -> none
    all_to_all x2 -> x1, blocking collectives: 30.3 us -> 24.3 us  [from_all(): return lax.all_to_all(spread, axes, split_axis=0, concat_axis=0, tiled=True)]
    ppermute x0 -> x3, waiting for transfers between devices: none -> 3.74 us  [sum_everywhere(): arrived.append(lax.ppermute(value, axes, pairs))]
    ppermute x2, starting transfers between devices: 9.36 us -> 7.35 us  [swap_cores(): return lax.ppermute(value, 'c', [(0, 1), (1, 0)])]
    pallas_call x1, Pallas kernels: 3.95 us -> 2.08 us  [shards(): pl.pallas_call(functools.partial(unpack_kernel, utterances), out_shape=(j...]
    pallas_call x1, Pallas kernels: 9.26 us -> 7.43 us  [local_grads(): pl.pallas_call(joint_kernel, out_shape=(pltpu.VMEM((3 * width * width //...]
  transfers between devices with their start and end apart: 2 -> 5, of which waited for: 2 -> 4; matrix products, arithmetic and copies ran while one was open for 0% -> 0% of each run, Pallas kernels for 0% -> 0%
where the time goes in v2:
time: 88.5 us; the launch traced here: 88.3 us
  blocking collectives  52.1 us (59%)
  starting transfers between devices  15.8 us (18%)
  waiting for transfers between devices  9.81 us (11%)
  Pallas kernels  9.51 us (11%)
    all_to_all x1, blocking collectives, sum_at_owner(): lax.all_to_all(value, axes, split_axis=0, concat_axis=0, tiled=True)  27.8 us
    all_to_all x1, blocking collectives, from_all(): return lax.all_to_all(spread, axes, split_axis=0, concat_axis=0, tiled=True)  24.3 us
    ppermute x3, starting transfers between devices, sum_everywhere(): arrived.append(lax.ppermute(value, axes, pairs))  8.45 us
    pallas_call x1, Pallas kernels, local_grads(): pl.pallas_call(joint_kernel, out_shape=(pltpu.VMEM((3 * width * width //...  7.43 us
    ppermute x2, starting transfers between devices, swap_cores(): return lax.ppermute(value, 'c', [(0, 1), (1, 0)])  7.35 us
    ppermute x2, waiting for transfers between devices, swap_cores(): return lax.ppermute(value, 'c', [(0, 1), (1, 0)])  6.07 us
    ppermute x3, waiting for transfers between devices, sum_everywhere(): arrived.append(lax.ppermute(value, axes, pairs))  3.74 us
    pallas_call x1, Pallas kernels, shards(): pl.pallas_call(functools.partial(unpack_kernel, utterances), out_shape=(j...  2.08 us
  transfers between devices with their start and end apart: 5, of which 4 were waited for; matrix products, arithmetic and copies ran while one was open for 0% of the time, Pallas kernels for 0%

profile of v2, /device:TPU:1, one launch (start us, length us, event | category | flops | bytes accessed | tf_op | source)
XLA Modules:
  0.0 88.3 jit_solution(1598959962770579439)
XLA Ops:
  0.6 7.4 %joint.1 = (f32[3072,128]{1,0:T(8,128)S(1)}, f32[3072,128]{1,0:T(8,128)S(1)}) custom-call(s32[4]{0:T(128)} %frames_hbm.1, s32[4]{0:T(128)} %lens_hbm.1, bf16[128,512]{1,0:T(8,128)(2,1)} %bitcast.13, bf16[17,4,512]{2,1,0:T(4,128)(2,1)} %bitcast.14, bf16[512,512]{1,0:T(8,128)(2,1)} %w_enc_hbm.1, bf16[512,512]{1,0:T(8,128)(2,1)} %w_pred_hbm.1, ...), custom_call_target="tpu_custom_call" | custom-call | tf_op jit(solution)/shard_map/joint/pallas_call | solution.py:312
  8.1 3.3 %collective-permute-start = (f32[3072,128]{1,0:T(8,128)S(1)}, f32[3072,128]{1,0:T(8,128)S(1)}, u32[]{:S(2)}, u32[]{:S(2)}) collective-permute-start(f32[3072,128]{1,0:T(8,128)S(1)} %get-tuple-element.13), channel_id=1, source_target_pairs={{0,1},{1,0},{2,3},{3,2},{4,5},{5,4},{6,7},{7,6},{8,9},{9,8},{10,11... | collective-permute-start | bytes 4718600 | tf_op jit(solution)/shard_map/ppermute | solution.py:387
  11.4 3.0 %collective-permute-done = f32[3072,128]{1,0:T(8,128)S(1)} collective-permute-done((f32[3072,128]{1,0:T(8,128)S(1)}, f32[3072,128]{1,0:T(8,128)S(1)}, u32[]{:S(2)}, u32[]{:S(2)}) %collective-permute-start) | collective-permute-done | bytes 1572896 | tf_op jit(solution)/shard_map/ppermute | solution.py:387
  14.4 0.2 add.12
  14.6 27.8 %all_to_all.17 = f32[32,96,128]{2,1,0:T(8,128)S(1)} all-to-all(f32[32,96,128]{2,1,0:T(8,128)S(1)} %bitcast.11), channel_id=1, replica_groups=mesh['zq'=2,'zp'=2,'x'=4,'y'=4,'zh'=2,'c'=2] {'zp','x','y'}, dimensions={0} | all-to-all | bytes 3145728 | tf_op jit(solution)/shard_map/all_to_all | solution.py:392
  42.4 0.1 reduce_sum.9
  42.5 5.2 %collective-permute-start.3 = (f32[96,128]{1,0:T(8,128)S(1)}, f32[96,128]{1,0:T(8,128)S(1)}, u32[]{:S(2)}, u32[]{:S(2)}) collective-permute-start(f32[96,128]{1,0:T(8,128)S(1)} %reduce_sum.9), channel_id=1, source_target_pairs={{0,130},{128,0},{2,128},{130,2},{1,131},{129,1},{3,129},{131,3},{4... | collective-permute-start | bytes 147464 | tf_op jit(solution)/shard_map/ppermute | solution.py:412
  47.7 0.0 collective-permute-start.2
  47.7 3.2 %collective-permute-start.1 = (f32[96,128]{1,0:T(8,128)S(1)}, f32[96,128]{1,0:T(8,128)S(1)}, u32[]{:S(2)}, u32[]{:S(2)}) collective-permute-start(f32[96,128]{1,0:T(8,128)S(1)} %reduce_sum.9), channel_id=1, source_target_pairs={{0,2},{128,130},{2,0},{130,128},{1,3},{129,131},{3,1},{131,129},{4... | collective-permute-start | bytes 147464 | tf_op jit(solution)/shard_map/ppermute | solution.py:412
  50.9 0.0 collective-permute-done.3
  50.9 2.4 %collective-permute-done.2 = f32[96,128]{1,0:T(8,128)S(1)} collective-permute-done((f32[96,128]{1,0:T(8,128)S(1)}, f32[96,128]{1,0:T(8,128)S(1)}, u32[]{:S(2)}, u32[]{:S(2)}) %collective-permute-start.2) | collective-permute-done | bytes 49184 | tf_op jit(solution)/shard_map/ppermute | solution.py:412
  53.3 1.4 %collective-permute-done.1 = f32[96,128]{1,0:T(8,128)S(1)} collective-permute-done((f32[96,128]{1,0:T(8,128)S(1)}, f32[96,128]{1,0:T(8,128)S(1)}, u32[]{:S(2)}, u32[]{:S(2)}) %collective-permute-start.1) | collective-permute-done | bytes 49184 | tf_op jit(solution)/shard_map/ppermute | solution.py:412
  54.7 0.2 broadcast_in_dim.2
  54.9 24.3 %all_to_all.18 = f32[32,96,128]{2,1,0:T(8,128)S(1)} all-to-all(f32[32,96,128]{2,1,0:T(8,128)S(1)} %broadcast_in_dim.2), channel_id=1, replica_groups=mesh['zq'=2,'zp'=2,'x'=4,'y'=4,'zh'=2,'c'=2] {'zp','x','y'}, dimensions={0} | all-to-all | bytes 3145728 | tf_op jit(solution)/shard_map/all_to_all | solution.py:400
  79.2 4.1 %collective-permute-start.4 = (f32[3072,128]{1,0:T(8,128)S(1)}, f32[3072,128]{1,0:T(8,128)S(1)}, u32[]{:S(2)}, u32[]{:S(2)}) collective-permute-start(f32[3072,128]{1,0:T(8,128)S(1)} %bitcast.9), channel_id=1, source_target_pairs={{0,1},{1,0},{2,3},{3,2},{4,5},{5,4},{6,7},{7,6},{8,9},{9,8},{10,11... | collective-permute-start | bytes 4718600 | tf_op jit(solution)/shard_map/ppermute | solution.py:387
  83.2 3.0 %collective-permute-done.4.other_ref = f32[3072,128]{1,0:T(8,128)S(1)} collective-permute-done((f32[3072,128]{1,0:T(8,128)S(1)}, f32[3072,128]{1,0:T(8,128)S(1)}, u32[]{:S(2)}, u32[]{:S(2)}) %collective-permute-start.4) | collective-permute-done | bytes 1572896 | tf_op jit(solution)/shard_map/ppermute | solution.py:387
  86.2 2.1 %unpack.1 = (f32[512,512]{1,0:T(8,128)}, f32[512,512]{1,0:T(8,128)}, f32[500,512]{1,0:T(8,128)}, f32[1,500]{1,0:T(1,128)}, f32[1,1]{1,0:T(1,128)}) custom-call(f32[3072,128]{1,0:T(8,128)S(1)} %bitcast.10, f32[3072,128]{1,0:T(8,128)S(1)} %collective-permute-done.4.other_ref), custom_call_target="tpu_custom_call" | custom-call | tf_op jit(solution)/shard_map/unpack/pallas_call | solution.py:426
  (1 shorter events, 0.0 us)
Async XLA Ops:
  8.1 6.3 %collective-permute-start = (f32[3072,128]{1,0:T(8,128)S(1)}, f32[3072,128]{1,0:T(8,128)S(1)}, u32[]{:S(2)}, u32[]{:S(2)}) collective-permute-start(f32[3072,128]{1,0:T(8,128)S(1)} %get-tuple-element.13), channel_id=1, source_target_pairs={{0,1},{1,0},{2,3},{3,2},{4,5},{5,4},{6,7},{7,6},{8,9},{9,8},{10,11... | collective-permute-start | bytes 4718600 | tf_op jit(solution)/shard_map/ppermute | solution.py:387
  42.5 8.4 %collective-permute-start.3 = (f32[96,128]{1,0:T(8,128)S(1)}, f32[96,128]{1,0:T(8,128)S(1)}, u32[]{:S(2)}, u32[]{:S(2)}) collective-permute-start(f32[96,128]{1,0:T(8,128)S(1)} %reduce_sum.9), channel_id=1, source_target_pairs={{0,130},{128,0},{2,128},{130,2},{1,131},{129,1},{3,129},{131,3},{4... | collective-permute-start | bytes 147464 | tf_op jit(solution)/shard_map/ppermute | solution.py:412
  47.7 5.6 %collective-permute-start.2 = (f32[96,128]{1,0:T(8,128)S(1)}, f32[96,128]{1,0:T(8,128)S(1)}, u32[]{:S(2)}, u32[]{:S(2)}) collective-permute-start(f32[96,128]{1,0:T(8,128)S(1)} %reduce_sum.9), channel_id=1, source_target_pairs={{0,128},{128,2},{2,130},{130,0},{1,129},{129,3},{3,131},{131,1},{4... | collective-permute-start | bytes 147464 | tf_op jit(solution)/shard_map/ppermute | solution.py:412
  47.7 7.0 %collective-permute-start.1 = (f32[96,128]{1,0:T(8,128)S(1)}, f32[96,128]{1,0:T(8,128)S(1)}, u32[]{:S(2)}, u32[]{:S(2)}) collective-permute-start(f32[96,128]{1,0:T(8,128)S(1)} %reduce_sum.9), channel_id=1, source_target_pairs={{0,2},{128,130},{2,0},{130,128},{1,3},{129,131},{3,1},{131,129},{4... | collective-permute-start | bytes 147464 | tf_op jit(solution)/shard_map/ppermute | solution.py:412
  79.2 7.1 %collective-permute-start.4 = (f32[3072,128]{1,0:T(8,128)S(1)}, f32[3072,128]{1,0:T(8,128)S(1)}, u32[]{:S(2)}, u32[]{:S(2)}) collective-permute-start(f32[3072,128]{1,0:T(8,128)S(1)} %bitcast.9), channel_id=1, source_target_pairs={{0,1},{1,0},{2,3},{3,2},{4,5},{5,4},{6,7},{7,6},{8,9},{9,8},{10,11... | collective-permute-start | bytes 4718600 | tf_op jit(solution)/shard_map/ppermute | solution.py:387

commit v3 on v2

--- a/solution.py
+++ b/solution.py
@@ -15,6 +15,8 @@
 AXES = ("zq", "zp", "x", "y", "zh", "c")
 NEAR = ("zp", "x", "y")
 FAR = ("zq", "zh")
+SECOND = 0
+STAGGER = 900
 PAIRS = tuple((j, s) for s in range(S) for j in range(s + 1))
 
 
@@ -383,6 +385,29 @@
         place((other_ref, mine_ref))
 
 
+def merge_kernel(keep_ref, recv_ref, out_ref):
+    out_ref[...] = keep_ref[...] + recv_ref[...]
+
+    @pl.when(lax.axis_index("c") == SECOND)
+    def _():
+        spare = out_ref.shape[0] - 8
+        first = out_ref[spare:, :]
+        out_ref[spare:, :] = lax.fori_loop(0, STAGGER, lambda _, v: jnp.tanh(v), first)
+
+
+def merge(keep, recv):
+    vmem = pl.BlockSpec(memory_space=pltpu.VMEM)
+    return pl.pallas_call(
+        merge_kernel,
+        out_shape=pltpu.VMEM(keep.shape, F32),
+        in_specs=[vmem, vmem],
+        out_specs=vmem,
+        input_output_aliases={0: 0},
+        compiler_params=pltpu.CompilerParams(vmem_limit_bytes=8 * 2**20),
+        name="merge",
+    )(keep, recv)
+
+
 def swap_cores(value):
     return lax.ppermute(value, "c", [(0, 1), (1, 0)])
 
@@ -415,7 +440,7 @@
 
 def shards(*args):
     keep, send = local_grads(*args)
-    mine = keep + swap_cores(send)
+    mine = merge(keep, swap_cores(send))
     mine = sum_at_owner(mine, NEAR)
     mine = sum_everywhere(mine, FAR)
     mine = from_all(mine, NEAR)

time: 88.5 us -> 84.7 us (0.957)
  blocking collectives: 52.1 us -> 41.8 us
  starting transfers between devices: 15.8 us -> 22.3 us
    ppermute x2, starting transfers between devices: 7.35 us -> 13.9 us  [swap_cores(): return lax.ppermute(value, 'c', [(0, 1), (1, 0)])]
    all_to_all x1, blocking collectives: 24.3 us -> 18.8 us  [from_all(): return lax.all_to_all(spread, axes, split_axis=0, concat_axis=0, tiled=True)]
    all_to_all x1, blocking collectives: 27.8 us -> 23 us  [sum_at_owner(): lax.all_to_all(value, axes, split_axis=0, concat_axis=0, tiled=True)]
where the time goes in v3:
time: 84.7 us; the launch traced here: 84.5 us
  blocking collectives  41.8 us (49%)
  starting transfers between devices  22.3 us (26%)
  Pallas kernels  9.78 us (12%)
  waiting for transfers between devices  9.67 us (11%)
    all_to_all x1, blocking collectives, sum_at_owner(): lax.all_to_all(value, axes, split_axis=0, concat_axis=0, tiled=True)  23 us
    all_to_all x1, blocking collectives, from_all(): return lax.all_to_all(spread, axes, split_axis=0, concat_axis=0, tiled=True)  18.8 us
    ppermute x2, starting transfers between devices, swap_cores(): return lax.ppermute(value, 'c', [(0, 1), (1, 0)])  13.9 us
    ppermute x3, starting transfers between devices, sum_everywhere(): arrived.append(lax.ppermute(value, axes, pairs))  8.45 us
    pallas_call x1, Pallas kernels, local_grads(): pl.pallas_call(joint_kernel, out_shape=(pltpu.VMEM((3 * width * width //...  7.43 us
    ppermute x2, waiting for transfers between devices, swap_cores(): return lax.ppermute(value, 'c', [(0, 1), (1, 0)])  6.07 us
    ppermute x3, waiting for transfers between devices, sum_everywhere(): arrived.append(lax.ppermute(value, axes, pairs))  3.6 us
    pallas_call x1, Pallas kernels, shards(): pl.pallas_call(functools.partial(unpack_kernel, utterances), out_shape=(j...  2.08 us
  transfers between devices with their start and end apart: 5, of which 4 were waited for; matrix products, arithmetic and copies ran while one was open for 0% of the time, Pallas kernels for 0%

profile of v3, /device:TPU:1, one launch (start us, length us, event | category | flops | bytes accessed | tf_op | source)
XLA Modules:
  0.0 84.5 jit_solution(8551832317202756882)
XLA Ops:
  0.6 7.4 %joint.1 = (f32[3072,128]{1,0:T(8,128)S(1)}, f32[3072,128]{1,0:T(8,128)S(1)}) custom-call(s32[4]{0:T(128)} %frames_hbm.1, s32[4]{0:T(128)} %lens_hbm.1, bf16[128,512]{1,0:T(8,128)(2,1)} %bitcast.13, bf16[17,4,512]{2,1,0:T(4,128)(2,1)} %bitcast.14, bf16[512,512]{1,0:T(8,128)(2,1)} %w_enc_hbm.1, bf16[512,512]{1,0:T(8,128)(2,1)} %w_pred_hbm.1, ...), custom_call_target="tpu_custom_call" | custom-call | tf_op jit(solution)/shard_map/joint/pallas_call | solution.py:314
  8.1 3.3 %collective-permute-start = (f32[3072,128]{1,0:T(8,128)S(1)}, f32[3072,128]{1,0:T(8,128)S(1)}, u32[]{:S(2)}, u32[]{:S(2)}) collective-permute-start(f32[3072,128]{1,0:T(8,128)S(1)} %get-tuple-element.13), channel_id=1, source_target_pairs={{0,1},{1,0},{2,3},{3,2},{4,5},{5,4},{6,7},{7,6},{8,9},{9,8},{10,11... | collective-permute-start | bytes 4718600 | tf_op jit(solution)/shard_map/ppermute | solution.py:412
  11.4 3.0 %collective-permute-done.recv_ref = f32[3072,128]{1,0:T(8,128)S(1)} collective-permute-done((f32[3072,128]{1,0:T(8,128)S(1)}, f32[3072,128]{1,0:T(8,128)S(1)}, u32[]{:S(2)}, u32[]{:S(2)}) %collective-permute-start) | collective-permute-done | bytes 1572896 | tf_op jit(solution)/shard_map/ppermute | solution.py:412
  14.4 0.3 merge.1
  14.7 23.0 %all_to_all.17 = f32[32,96,128]{2,1,0:T(8,128)S(1)} all-to-all(f32[32,96,128]{2,1,0:T(8,128)S(1)} %bitcast.11), channel_id=1, replica_groups=mesh['zq'=2,'zp'=2,'x'=4,'y'=4,'zh'=2,'c'=2] {'zp','x','y'}, dimensions={0} | all-to-all | bytes 3145728 | tf_op jit(solution)/shard_map/all_to_all | solution.py:417
  37.7 0.1 reduce_sum.9
  37.8 5.2 %collective-permute-start.3 = (f32[96,128]{1,0:T(8,128)S(1)}, f32[96,128]{1,0:T(8,128)S(1)}, u32[]{:S(2)}, u32[]{:S(2)}) collective-permute-start(f32[96,128]{1,0:T(8,128)S(1)} %reduce_sum.9), channel_id=1, source_target_pairs={{0,130},{128,0},{2,128},{130,2},{1,131},{129,1},{3,129},{131,3},{4... | collective-permute-start | bytes 147464 | tf_op jit(solution)/shard_map/ppermute | solution.py:437
  43.0 0.0 collective-permute-start.2
  43.0 3.2 %collective-permute-start.1 = (f32[96,128]{1,0:T(8,128)S(1)}, f32[96,128]{1,0:T(8,128)S(1)}, u32[]{:S(2)}, u32[]{:S(2)}) collective-permute-start(f32[96,128]{1,0:T(8,128)S(1)} %reduce_sum.9), channel_id=1, source_target_pairs={{0,2},{128,130},{2,0},{130,128},{1,3},{129,131},{3,1},{131,129},{4... | collective-permute-start | bytes 147464 | tf_op jit(solution)/shard_map/ppermute | solution.py:437
  46.3 0.0 collective-permute-done.3
  46.3 1.8 %collective-permute-done.2 = f32[96,128]{1,0:T(8,128)S(1)} collective-permute-done((f32[96,128]{1,0:T(8,128)S(1)}, f32[96,128]{1,0:T(8,128)S(1)}, u32[]{:S(2)}, u32[]{:S(2)}) %collective-permute-start.2) | collective-permute-done | bytes 49184 | tf_op jit(solution)/shard_map/ppermute | solution.py:437
  48.1 1.8 %collective-permute-done.1 = f32[96,128]{1,0:T(8,128)S(1)} collective-permute-done((f32[96,128]{1,0:T(8,128)S(1)}, f32[96,128]{1,0:T(8,128)S(1)}, u32[]{:S(2)}, u32[]{:S(2)}) %collective-permute-start.1) | collective-permute-done | bytes 49184 | tf_op jit(solution)/shard_map/ppermute | solution.py:437
  49.9 0.2 broadcast_in_dim.2
  50.1 18.8 %all_to_all.18 = f32[32,96,128]{2,1,0:T(8,128)S(1)} all-to-all(f32[32,96,128]{2,1,0:T(8,128)S(1)} %broadcast_in_dim.2), channel_id=1, replica_groups=mesh['zq'=2,'zp'=2,'x'=4,'y'=4,'zh'=2,'c'=2] {'zp','x','y'}, dimensions={0} | all-to-all | bytes 3145728 | tf_op jit(solution)/shard_map/all_to_all | solution.py:425
  68.8 10.6 %collective-permute-start.4 = (f32[3072,128]{1,0:T(8,128)S(1)}, f32[3072,128]{1,0:T(8,128)S(1)}, u32[]{:S(2)}, u32[]{:S(2)}) collective-permute-start(f32[3072,128]{1,0:T(8,128)S(1)} %bitcast.9), channel_id=1, source_target_pairs={{0,1},{1,0},{2,3},{3,2},{4,5},{5,4},{6,7},{7,6},{8,9},{9,8},{10,11... | collective-permute-start | bytes 4718600 | tf_op jit(solution)/shard_map/ppermute | solution.py:412
  79.4 3.0 %collective-permute-done.4.other_ref = f32[3072,128]{1,0:T(8,128)S(1)} collective-permute-done((f32[3072,128]{1,0:T(8,128)S(1)}, f32[3072,128]{1,0:T(8,128)S(1)}, u32[]{:S(2)}, u32[]{:S(2)}) %collective-permute-start.4) | collective-permute-done | bytes 1572896 | tf_op jit(solution)/shard_map/ppermute | solution.py:412
  82.4 2.1 %unpack.1 = (f32[512,512]{1,0:T(8,128)}, f32[512,512]{1,0:T(8,128)}, f32[500,512]{1,0:T(8,128)}, f32[1,500]{1,0:T(1,128)}, f32[1,1]{1,0:T(1,128)}) custom-call(f32[3072,128]{1,0:T(8,128)S(1)} %bitcast.10, f32[3072,128]{1,0:T(8,128)S(1)} %collective-permute-done.4.other_ref), custom_call_target="tpu_custom_call" | custom-call | tf_op jit(solution)/shard_map/unpack/pallas_call | solution.py:451
  (1 shorter events, 0.0 us)
Async XLA Ops:
  8.1 6.3 %collective-permute-start = (f32[3072,128]{1,0:T(8,128)S(1)}, f32[3072,128]{1,0:T(8,128)S(1)}, u32[]{:S(2)}, u32[]{:S(2)}) collective-permute-start(f32[3072,128]{1,0:T(8,128)S(1)} %get-tuple-element.13), channel_id=1, source_target_pairs={{0,1},{1,0},{2,3},{3,2},{4,5},{5,4},{6,7},{7,6},{8,9},{9,8},{10,11... | collective-permute-start | bytes 4718600 | tf_op jit(solution)/shard_map/ppermute | solution.py:412
  37.8 8.4 %collective-permute-start.3 = (f32[96,128]{1,0:T(8,128)S(1)}, f32[96,128]{1,0:T(8,128)S(1)}, u32[]{:S(2)}, u32[]{:S(2)}) collective-permute-start(f32[96,128]{1,0:T(8,128)S(1)} %reduce_sum.9), channel_id=1, source_target_pairs={{0,130},{128,0},{2,128},{130,2},{1,131},{129,1},{3,129},{131,3},{4... | collective-permute-start | bytes 147464 | tf_op jit(solution)/shard_map/ppermute | solution.py:437
  43.0 5.1 %collective-permute-start.2 = (f32[96,128]{1,0:T(8,128)S(1)}, f32[96,128]{1,0:T(8,128)S(1)}, u32[]{:S(2)}, u32[]{:S(2)}) collective-permute-start(f32[96,128]{1,0:T(8,128)S(1)} %reduce_sum.9), channel_id=1, source_target_pairs={{0,128},{128,2},{2,130},{130,0},{1,129},{129,3},{3,131},{131,1},{4... | collective-permute-start | bytes 147464 | tf_op jit(solution)/shard_map/ppermute | solution.py:437
  43.0 6.8 %collective-permute-start.1 = (f32[96,128]{1,0:T(8,128)S(1)}, f32[96,128]{1,0:T(8,128)S(1)}, u32[]{:S(2)}, u32[]{:S(2)}) collective-permute-start(f32[96,128]{1,0:T(8,128)S(1)} %reduce_sum.9), channel_id=1, source_target_pairs={{0,2},{128,130},{2,0},{130,128},{1,3},{129,131},{3,1},{131,129},{4... | collective-permute-start | bytes 147464 | tf_op jit(solution)/shard_map/ppermute | solution.py:437
  68.8 13.6 %collective-permute-start.4 = (f32[3072,128]{1,0:T(8,128)S(1)}, f32[3072,128]{1,0:T(8,128)S(1)}, u32[]{:S(2)}, u32[]{:S(2)}) collective-permute-start(f32[3072,128]{1,0:T(8,128)S(1)} %bitcast.9), channel_id=1, source_target_pairs={{0,1},{1,0},{2,3},{3,2},{4,5},{5,4},{6,7},{7,6},{8,9},{9,8},{10,11... | collective-permute-start | bytes 4718600 | tf_op jit(solution)/shard_map/ppermute | solution.py:412

commit v4 on v3

--- a/solution.py
+++ b/solution.py
@@ -354,35 +354,67 @@
     )
 
 
-def unpack_kernel(utterances, mine_ref, other_ref, enc_ref, pred_ref, joint_ref, bias_ref, loss_ref):
+def place_kernel(utterances, sides, *refs):
+    half_ref, others = refs[0], refs[1:]
+    enc_ref, pred_ref, joint_ref, bias_ref, loss_ref, sems = others[-6:]
     core = lax.axis_index("c")
     width = enc_ref.shape[0]
     vocab = joint_ref.shape[0]
-    half = width // 256
-
-    def place(refs):
-        for h in range(2):
-            for m, out_ref in enumerate((enc_ref, pred_ref, joint_ref)):
-                for j in range(half):
-                    at = (m * half + j) * width
-                    lane = (h * half + j) * 128
-                    size = out_ref.shape[0]
-                    out_ref[:, lane : lane + 128] = refs[h][at : at + size, :]
-            for j in range(half):
-                at = (2 * half + j) * width + vocab
-                lane = (h * half + j) * 128
-                size = min(128, vocab - lane)
-                bias_ref[:, lane : lane + size] = refs[h][at : at + 1, :size]
-        at = 2 * half * width + vocab + 1
-        loss_ref[...] = refs[0][at : at + 1, 0:1] / utterances
-
-    @pl.when(core == 0)
-    def _():
-        place((mine_ref, other_ref))
-
-    @pl.when(core != 0)
-    def _():
-        place((other_ref, mine_ref))
+    tiles = width // 256
+    outs = (enc_ref, pred_ref, joint_ref)
+
+    def place(h):
+        copies = []
+        for m, out_ref in enumerate(outs):
+            size = out_ref.shape[0]
+            for j in range(tiles):
+                lane = (h * tiles + j) * 128
+                copies.append(
+                    pltpu.make_async_copy(
+                        half_ref.at[pl.ds((m * tiles + j) * width, size), :],
+                        out_ref.at[:, pl.ds(lane, 128)],
+                        sems.at[m * tiles + j],
+                    )
+                )
+        for copy in copies:
+            copy.start()
+        if sides:
+            bias_ref[...] = others[3][...]
+        for j in range(tiles):
+            at = (2 * tiles + j) * width + vocab
+            lane = (h * tiles + j) * 128
+            size = min(128, vocab - lane)
+            bias_ref[:, lane : lane + size] = half_ref[at : at + 1, :size]
+        at = 2 * tiles * width + vocab + 1
+        loss_ref[...] = half_ref[at : at + 1, 0:1] / utterances
+        for copy in copies:
+            copy.wait()
+
+    for h in range(2):
+        @pl.when((core + sides) % 2 == h)
+        def _():
+            place(h)
+
+
+def place(half, so_far, utterances, shapes):
+    vmem = pl.BlockSpec(memory_space=pltpu.VMEM)
+    hbm = pl.BlockSpec(memory_space=pltpu.HBM)
+    big, small = shapes[:3], shapes[3:]
+    out_shape = [pltpu.HBM(d, F32) for d in big] + [jax.ShapeDtypeStruct(d, F32) for d in small]
+    inputs = (half, *so_far[:4])
+    return pl.pallas_call(
+        functools.partial(place_kernel, utterances, int(bool(so_far))),
+        out_shape=out_shape,
+        in_specs=[vmem] + ([hbm] * 3 + [vmem] if so_far else []),
+        out_specs=[hbm] * 3 + [vmem] * 2,
+        scratch_shapes=[pltpu.SemaphoreType.DMA((6,))],
+        input_output_aliases={1: 0, 2: 1, 3: 2} if so_far else {},
+        compiler_params=pltpu.CompilerParams(vmem_limit_bytes=8 * 2**20),
+        cost_estimate=pl.CostEstimate(
+            flops=2**24, bytes_accessed=2 * half.size * 4, transcendentals=0
+        ),
+        name="place",
+    )(*inputs)
 
 
 def merge_kernel(keep_ref, recv_ref, out_ref):
@@ -447,21 +479,11 @@
     other = swap_cores(mine)
     width, vocab = args[4].shape
     utterances = args[0].shape[0] * lax.axis_size(AXES)
-    vmem = pl.BlockSpec(memory_space=pltpu.VMEM)
-    grad_encoder, grad_predictor, grad_joint, grad_bias, loss = pl.pallas_call(
-        functools.partial(unpack_kernel, utterances),
-        out_shape=(
-            jax.ShapeDtypeStruct((width, width), F32),
-            jax.ShapeDtypeStruct((width, width), F32),
-            jax.ShapeDtypeStruct((vocab, width), F32),
-            jax.ShapeDtypeStruct((1, vocab), F32),
-            jax.ShapeDtypeStruct((1, 1), F32),
-        ),
-        in_specs=[vmem, vmem],
-        out_specs=(vmem,) * 5,
-        compiler_params=pltpu.CompilerParams(vmem_limit_bytes=20 * 2**20),
-        name="unpack",
-    )(mine, other)
+    shapes = ((width, width), (width, width), (vocab, width), (1, vocab), (1, 1))
+    so_far = place(mine, (), utterances, shapes)
+    grad_encoder, grad_predictor, grad_joint, grad_bias, loss = place(
+        other, so_far, utterances, shapes
+    )
     return grad_encoder, grad_predictor, grad_joint.T, grad_bias.reshape(vocab), loss.reshape(())
 
 

time: 84.7 us -> 84.4 us (level)
  waiting for transfers between devices: 9.67 us -> 7.98 us
  Pallas kernels: 9.78 us -> 11.2 us
    ppermute x2, waiting for transfers between devices: 6.07 us -> 4.38 us  [swap_cores(): return lax.ppermute(value, 'c', [(0, 1), (1, 0)])]
    pallas_call x1 -> x2, Pallas kernels: 2.08 us -> 3.45 us  [place(): pl.pallas_call(functools.partial(place_kernel, utterances, int(bool(so_fa...]
  transfers between devices with their start and end apart: 5 -> 5, of which waited for: 4 -> 4; matrix products, arithmetic and copies ran while one was open for 0% -> 0% of each run, Pallas kernels for 0% -> 2%
where the time goes in v4:
time: 84.4 us; the launch traced here: 84.2 us
  blocking collectives  41.8 us (50%)
  starting transfers between devices  22.3 us (26%)
  Pallas kernels  11.2 us (13%)
  waiting for transfers between devices  7.98 us (9%)
    all_to_all x1, blocking collectives, sum_at_owner(): lax.all_to_all(value, axes, split_axis=0, concat_axis=0, tiled=True)  23 us
    all_to_all x1, blocking collectives, from_all(): return lax.all_to_all(spread, axes, split_axis=0, concat_axis=0, tiled=True)  18.8 us
    ppermute x2, starting transfers between devices, swap_cores(): return lax.ppermute(value, 'c', [(0, 1), (1, 0)])  13.9 us
    ppermute x3, starting transfers between devices, sum_everywhere(): arrived.append(lax.ppermute(value, axes, pairs))  8.45 us
    pallas_call x1, Pallas kernels, local_grads(): pl.pallas_call(joint_kernel, out_shape=(pltpu.VMEM((3 * width * width //...  7.43 us
    ppermute x2, waiting for transfers between devices, swap_cores(): return lax.ppermute(value, 'c', [(0, 1), (1, 0)])  4.38 us
    ppermute x3, waiting for transfers between devices, sum_everywhere(): arrived.append(lax.ppermute(value, axes, pairs))  3.6 us
    pallas_call x2, Pallas kernels, place(): pl.pallas_call(functools.partial(place_kernel, utterances, int(bool(so_fa...  3.45 us
  transfers between devices with their start and end apart: 5, of which 4 were waited for; matrix products, arithmetic and copies ran while one was open for 0% of the time, Pallas kernels for 2%

profile of v4, /device:TPU:1, one launch (start us, length us, event | category | flops | bytes accessed | tf_op | source)
XLA Modules:
  0.0 84.2 jit_solution(15059624204344736985)
XLA Ops:
  0.6 7.4 %joint.1 = (f32[3072,128]{1,0:T(8,128)S(1)}, f32[3072,128]{1,0:T(8,128)S(1)}) custom-call(s32[4]{0:T(128)} %frames_hbm.1, s32[4]{0:T(128)} %lens_hbm.1, bf16[128,512]{1,0:T(8,128)(2,1)} %bitcast.14, bf16[17,4,512]{2,1,0:T(4,128)(2,1)} %bitcast.15, bf16[512,512]{1,0:T(8,128)(2,1)} %w_enc_hbm.1, bf16[512,512]{1,0:T(8,128)(2,1)} %w_pred_hbm.1, ...), custom_call_target="tpu_custom_call" | custom-call | tf_op jit(solution)/shard_map/joint/pallas_call | solution.py:314
  8.1 3.3 %collective-permute-start = (f32[3072,128]{1,0:T(8,128)S(1)}, f32[3072,128]{1,0:T(8,128)S(1)}, u32[]{:S(2)}, u32[]{:S(2)}) collective-permute-start(f32[3072,128]{1,0:T(8,128)S(1)} %get-tuple-element.17), channel_id=1, source_target_pairs={{0,1},{1,0},{2,3},{3,2},{4,5},{5,4},{6,7},{7,6},{8,9},{9,8},{10,11... | collective-permute-start | bytes 4718600 | tf_op jit(solution)/shard_map/ppermute | solution.py:444
  11.4 3.0 %collective-permute-done.recv_ref = f32[3072,128]{1,0:T(8,128)S(1)} collective-permute-done((f32[3072,128]{1,0:T(8,128)S(1)}, f32[3072,128]{1,0:T(8,128)S(1)}, u32[]{:S(2)}, u32[]{:S(2)}) %collective-permute-start) | collective-permute-done | bytes 1572896 | tf_op jit(solution)/shard_map/ppermute | solution.py:444
  14.4 0.3 merge.1
  14.7 23.0 %all_to_all.17 = f32[32,96,128]{2,1,0:T(8,128)S(1)} all-to-all(f32[32,96,128]{2,1,0:T(8,128)S(1)} %bitcast.11), channel_id=1, replica_groups=mesh['zq'=2,'zp'=2,'x'=4,'y'=4,'zh'=2,'c'=2] {'zp','x','y'}, dimensions={0} | all-to-all | bytes 3145728 | tf_op jit(solution)/shard_map/all_to_all | solution.py:449
  37.7 0.1 reduce_sum.9
  37.8 5.2 %collective-permute-start.3 = (f32[96,128]{1,0:T(8,128)S(1)}, f32[96,128]{1,0:T(8,128)S(1)}, u32[]{:S(2)}, u32[]{:S(2)}) collective-permute-start(f32[96,128]{1,0:T(8,128)S(1)} %reduce_sum.9), channel_id=1, source_target_pairs={{0,130},{128,0},{2,128},{130,2},{1,131},{129,1},{3,129},{131,3},{4... | collective-permute-start | bytes 147464 | tf_op jit(solution)/shard_map/ppermute | solution.py:469
  43.0 0.0 collective-permute-start.2
  43.0 3.2 %collective-permute-start.1 = (f32[96,128]{1,0:T(8,128)S(1)}, f32[96,128]{1,0:T(8,128)S(1)}, u32[]{:S(2)}, u32[]{:S(2)}) collective-permute-start(f32[96,128]{1,0:T(8,128)S(1)} %reduce_sum.9), channel_id=1, source_target_pairs={{0,2},{128,130},{2,0},{130,128},{1,3},{129,131},{3,1},{131,129},{4... | collective-permute-start | bytes 147464 | tf_op jit(solution)/shard_map/ppermute | solution.py:469
  46.3 0.0 collective-permute-done.3
  46.3 1.8 %collective-permute-done.2 = f32[96,128]{1,0:T(8,128)S(1)} collective-permute-done((f32[96,128]{1,0:T(8,128)S(1)}, f32[96,128]{1,0:T(8,128)S(1)}, u32[]{:S(2)}, u32[]{:S(2)}) %collective-permute-start.2) | collective-permute-done | bytes 49184 | tf_op jit(solution)/shard_map/ppermute | solution.py:469
  48.1 1.8 %collective-permute-done.1 = f32[96,128]{1,0:T(8,128)S(1)} collective-permute-done((f32[96,128]{1,0:T(8,128)S(1)}, f32[96,128]{1,0:T(8,128)S(1)}, u32[]{:S(2)}, u32[]{:S(2)}) %collective-permute-start.1) | collective-permute-done | bytes 49184 | tf_op jit(solution)/shard_map/ppermute | solution.py:469
  49.9 0.2 broadcast_in_dim.2
  50.1 18.8 %all_to_all.18 = f32[32,96,128]{2,1,0:T(8,128)S(1)} all-to-all(f32[32,96,128]{2,1,0:T(8,128)S(1)} %broadcast_in_dim.2), channel_id=1, replica_groups=mesh['zq'=2,'zp'=2,'x'=4,'y'=4,'zh'=2,'c'=2] {'zp','x','y'}, dimensions={0} | all-to-all | bytes 3145728 | tf_op jit(solution)/shard_map/all_to_all | solution.py:457
  68.8 10.6 %collective-permute-start.4 = (f32[3072,128]{1,0:T(8,128)S(1)}, f32[3072,128]{1,0:T(8,128)S(1)}, u32[]{:S(2)}, u32[]{:S(2)}) collective-permute-start(f32[3072,128]{1,0:T(8,128)S(1)} %bitcast.9), channel_id=1, source_target_pairs={{0,1},{1,0},{2,3},{3,2},{4,5},{5,4},{6,7},{7,6},{8,9},{9,8},{10,11... | collective-permute-start | bytes 4718600 | tf_op jit(solution)/shard_map/ppermute | solution.py:444
  79.4 1.7 %place.2 = (f32[512,512]{1,0:T(8,128)}, f32[512,512]{1,0:T(8,128)}, f32[500,512]{1,0:T(8,128)}, f32[1,500]{1,0:T(1,128)S(1)}, f32[1,1]{1,0:T(1,128)}) custom-call(f32[3072,128]{1,0:T(8,128)S(1)} %bitcast.10), custom_call_target="tpu_custom_call" | custom-call | flops 16777216 | bytes 3145728 | tf_op jit(solution)/shard_map/place/pallas_call | solution.py:405
  81.1 1.3 %collective-permute-done.4.refs_0_ = f32[3072,128]{1,0:T(8,128)S(1)} collective-permute-done((f32[3072,128]{1,0:T(8,128)S(1)}, f32[3072,128]{1,0:T(8,128)S(1)}, u32[]{:S(2)}, u32[]{:S(2)}) %collective-permute-start.4) | collective-permute-done | bytes 1572896 | tf_op jit(solution)/shard_map/ppermute | solution.py:444
  82.4 1.8 %place.3 = (f32[512,512]{1,0:T(8,128)}, f32[512,512]{1,0:T(8,128)}, f32[500,512]{1,0:T(8,128)}, f32[1,500]{1,0:T(1,128)}, f32[1,1]{1,0:T(1,128)}) custom-call(f32[3072,128]{1,0:T(8,128)S(1)} %collective-permute-done.4.refs_0_, f32[512,512]{1,0:T(8,128)} %get-tuple-element.18.refs_1_, ...), custom_call_target="tpu_custom_call", output_to_operand_aliasing={{0}: (1, {}), {1}: (2, {}), {2}: (3, {})} | custom-call | flops 16777216 | bytes 3145728 | tf_op jit(solution)/shard_map/place/pallas_call | solution.py:405
  (1 shorter events, 0.0 us)
Async XLA Ops:
  8.1 6.3 %collective-permute-start = (f32[3072,128]{1,0:T(8,128)S(1)}, f32[3072,128]{1,0:T(8,128)S(1)}, u32[]{:S(2)}, u32[]{:S(2)}) collective-permute-start(f32[3072,128]{1,0:T(8,128)S(1)} %get-tuple-element.17), channel_id=1, source_target_pairs={{0,1},{1,0},{2,3},{3,2},{4,5},{5,4},{6,7},{7,6},{8,9},{9,8},{10,11... | collective-permute-start | bytes 4718600 | tf_op jit(solution)/shard_map/ppermute | solution.py:444
  37.8 8.4 %collective-permute-start.3 = (f32[96,128]{1,0:T(8,128)S(1)}, f32[96,128]{1,0:T(8,128)S(1)}, u32[]{:S(2)}, u32[]{:S(2)}) collective-permute-start(f32[96,128]{1,0:T(8,128)S(1)} %reduce_sum.9), channel_id=1, source_target_pairs={{0,130},{128,0},{2,128},{130,2},{1,131},{129,1},{3,129},{131,3},{4... | collective-permute-start | bytes 147464 | tf_op jit(solution)/shard_map/ppermute | solution.py:469
  43.0 5.1 %collective-permute-start.2 = (f32[96,128]{1,0:T(8,128)S(1)}, f32[96,128]{1,0:T(8,128)S(1)}, u32[]{:S(2)}, u32[]{:S(2)}) collective-permute-start(f32[96,128]{1,0:T(8,128)S(1)} %reduce_sum.9), channel_id=1, source_target_pairs={{0,128},{128,2},{2,130},{130,0},{1,129},{129,3},{3,131},{131,1},{4... | collective-permute-start | bytes 147464 | tf_op jit(solution)/shard_map/ppermute | solution.py:469
  43.0 6.8 %collective-permute-start.1 = (f32[96,128]{1,0:T(8,128)S(1)}, f32[96,128]{1,0:T(8,128)S(1)}, u32[]{:S(2)}, u32[]{:S(2)}) collective-permute-start(f32[96,128]{1,0:T(8,128)S(1)} %reduce_sum.9), channel_id=1, source_target_pairs={{0,2},{128,130},{2,0},{130,128},{1,3},{129,131},{3,1},{131,129},{4... | collective-permute-start | bytes 147464 | tf_op jit(solution)/shard_map/ppermute | solution.py:469
  68.8 13.6 %collective-permute-start.4 = (f32[3072,128]{1,0:T(8,128)S(1)}, f32[3072,128]{1,0:T(8,128)S(1)}, u32[]{:S(2)}, u32[]{:S(2)}) collective-permute-start(f32[3072,128]{1,0:T(8,128)S(1)} %bitcast.9), channel_id=1, source_target_pairs={{0,1},{1,0},{2,3},{3,2},{4,5},{5,4},{6,7},{7,6},{8,9},{9,8},{10,11... | collective-permute-start | bytes 4718600 | tf_op jit(solution)/shard_map/ppermute | solution.py:444

commit v5 on v4

--- a/solution.py
+++ b/solution.py
@@ -16,8 +16,15 @@
 NEAR = ("zp", "x", "y")
 FAR = ("zq", "zh")
 SECOND = 0
-STAGGER = 900
+STAGGER = 750
 PAIRS = tuple((j, s) for s in range(S) for j in range(s + 1))
+
+
+def tree(op, terms):
+    while len(terms) > 1:
+        pairs = [op(a, b) for a, b in zip(terms[::2], terms[1::2])]
+        terms = pairs + terms[len(terms) // 2 * 2 :]
+    return terms[0]
 
 
 def over_rows(a, b):
@@ -178,23 +185,17 @@
         emits = [emit_s[s, t : t + 1, :] for s in range(S - 1)]
         updated = []
         for s in range(S):
-            routes = []
-            for j in range(s + 1):
-                way = entering[j]
-                for i in range(j, s):
-                    way = way + emits[i]
-                routes.append(way)
-            best = routes[0]
-            for r in routes[1:]:
-                best = jnp.maximum(best, r)
+            routes = [
+                entering[j] + tree(jnp.add, emits[j:s]) if j < s else entering[j]
+                for j in range(s + 1)
+            ]
+            best = tree(jnp.maximum, routes)
             terms = [jnp.exp(r - best) for r in routes]
-            total = terms[0]
-            for r in terms[1:]:
-                total = total + r
+            total = tree(jnp.add, terms)
             for j in range(s + 1):
                 terms_s[PAIRS.index((j, s)), t : t + 1, :] = terms[j]
             sums_s[s, t : t + 1, :] = total
-            updated.append(best + jnp.log(total))
+            updated.append(best + jnp.log(total) if s else best)
         if t == 0:
             state = updated
         else:
@@ -230,10 +231,7 @@
         back = []
         for j in range(S):
             parts = [grads[s] * terms_s[PAIRS.index((j, s)), t : t + 1, :] for s in range(j, S)]
-            total = parts[0]
-            for r in parts[1:]:
-                total = total + r
-            back.append(total)
+            back.append(tree(jnp.add, parts))
         earlier = shifted(back, -shift_s[t : t + 1, :], -3, none)
         for s in range(S):
             gblank_s[s, t - 1 : t, :] += jnp.where(live, earlier[s], 0.0)

time: 84.4 us -> 84 us (level)
  starting transfers between devices: 22.3 us -> 21.2 us
    ppermute x2, starting transfers between devices: 13.9 us -> 12.7 us  [swap_cores(): return lax.ppermute(value, 'c', [(0, 1), (1, 0)])]
where the time goes in v5:
time: 84 us; the launch traced here: 83.8 us
  blocking collectives  42.5 us (51%)
  starting transfers between devices  21.2 us (25%)
  Pallas kernels  11.2 us (13%)
  waiting for transfers between devices  7.98 us (10%)
    all_to_all x1, blocking collectives, sum_at_owner(): lax.all_to_all(value, axes, split_axis=0, concat_axis=0, tiled=True)  23.6 us
    all_to_all x1, blocking collectives, from_all(): return lax.all_to_all(spread, axes, split_axis=0, concat_axis=0, tiled=True)  18.9 us
    ppermute x2, starting transfers between devices, swap_cores(): return lax.ppermute(value, 'c', [(0, 1), (1, 0)])  12.7 us
    ppermute x3, starting transfers between devices, sum_everywhere(): arrived.append(lax.ppermute(value, axes, pairs))  8.45 us
    pallas_call x1, Pallas kernels, local_grads(): pl.pallas_call(joint_kernel, out_shape=(pltpu.VMEM((3 * width * width //...  7.5 us
    ppermute x2, waiting for transfers between devices, swap_cores(): return lax.ppermute(value, 'c', [(0, 1), (1, 0)])  4.38 us
    ppermute x3, waiting for transfers between devices, sum_everywhere(): arrived.append(lax.ppermute(value, axes, pairs))  3.6 us
    pallas_call x2, Pallas kernels, place(): pl.pallas_call(functools.partial(place_kernel, utterances, int(bool(so_fa...  3.45 us
  transfers between devices with their start and end apart: 5, of which 4 were waited for; matrix products, arithmetic and copies ran while one was open for 0% of the time, Pallas kernels for 2%

profile of v5, /device:TPU:1, one launch (start us, length us, event | category | flops | bytes accessed | tf_op | source)
XLA Modules:
  0.0 83.8 jit_solution(16890549619022381871)
XLA Ops:
  0.6 7.5 %joint.1 = (f32[3072,128]{1,0:T(8,128)S(1)}, f32[3072,128]{1,0:T(8,128)S(1)}) custom-call(s32[4]{0:T(128)} %frames_hbm.1, s32[4]{0:T(128)} %lens_hbm.1, bf16[128,512]{1,0:T(8,128)(2,1)} %bitcast.14, bf16[17,4,512]{2,1,0:T(4,128)(2,1)} %bitcast.15, bf16[512,512]{1,0:T(8,128)(2,1)} %w_enc_hbm.1, bf16[512,512]{1,0:T(8,128)(2,1)} %w_pred_hbm.1, ...), custom_call_target="tpu_custom_call" | custom-call | tf_op jit(solution)/shard_map/joint/pallas_call | solution.py:312
  8.1 3.3 %collective-permute-start = (f32[3072,128]{1,0:T(8,128)S(1)}, f32[3072,128]{1,0:T(8,128)S(1)}, u32[]{:S(2)}, u32[]{:S(2)}) collective-permute-start(f32[3072,128]{1,0:T(8,128)S(1)} %get-tuple-element.17), channel_id=1, source_target_pairs={{0,1},{1,0},{2,3},{3,2},{4,5},{5,4},{6,7},{7,6},{8,9},{9,8},{10,11... | collective-permute-start | bytes 4718600 | tf_op jit(solution)/shard_map/ppermute | solution.py:442
  11.4 3.0 %collective-permute-done.recv_ref = f32[3072,128]{1,0:T(8,128)S(1)} collective-permute-done((f32[3072,128]{1,0:T(8,128)S(1)}, f32[3072,128]{1,0:T(8,128)S(1)}, u32[]{:S(2)}, u32[]{:S(2)}) %collective-permute-start) | collective-permute-done | bytes 1572896 | tf_op jit(solution)/shard_map/ppermute | solution.py:442
  14.5 0.3 merge.1
  14.7 23.6 %all_to_all.17 = f32[32,96,128]{2,1,0:T(8,128)S(1)} all-to-all(f32[32,96,128]{2,1,0:T(8,128)S(1)} %bitcast.11), channel_id=1, replica_groups=mesh['zq'=2,'zp'=2,'x'=4,'y'=4,'zh'=2,'c'=2] {'zp','x','y'}, dimensions={0} | all-to-all | bytes 3145728 | tf_op jit(solution)/shard_map/all_to_all | solution.py:447
  38.3 0.1 reduce_sum.9
  38.4 5.2 %collective-permute-start.3 = (f32[96,128]{1,0:T(8,128)S(1)}, f32[96,128]{1,0:T(8,128)S(1)}, u32[]{:S(2)}, u32[]{:S(2)}) collective-permute-start(f32[96,128]{1,0:T(8,128)S(1)} %reduce_sum.9), channel_id=1, source_target_pairs={{0,130},{128,0},{2,128},{130,2},{1,131},{129,1},{3,129},{131,3},{4... | collective-permute-start | bytes 147464 | tf_op jit(solution)/shard_map/ppermute | solution.py:467
  43.6 0.0 collective-permute-start.2
  43.6 3.2 %collective-permute-start.1 = (f32[96,128]{1,0:T(8,128)S(1)}, f32[96,128]{1,0:T(8,128)S(1)}, u32[]{:S(2)}, u32[]{:S(2)}) collective-permute-start(f32[96,128]{1,0:T(8,128)S(1)} %reduce_sum.9), channel_id=1, source_target_pairs={{0,2},{128,130},{2,0},{130,128},{1,3},{129,131},{3,1},{131,129},{4... | collective-permute-start | bytes 147464 | tf_op jit(solution)/shard_map/ppermute | solution.py:467
  46.9 0.0 collective-permute-done.3
  46.9 1.8 %collective-permute-done.2 = f32[96,128]{1,0:T(8,128)S(1)} collective-permute-done((f32[96,128]{1,0:T(8,128)S(1)}, f32[96,128]{1,0:T(8,128)S(1)}, u32[]{:S(2)}, u32[]{:S(2)}) %collective-permute-start.2) | collective-permute-done | bytes 49184 | tf_op jit(solution)/shard_map/ppermute | solution.py:467
  48.7 1.8 %collective-permute-done.1 = f32[96,128]{1,0:T(8,128)S(1)} collective-permute-done((f32[96,128]{1,0:T(8,128)S(1)}, f32[96,128]{1,0:T(8,128)S(1)}, u32[]{:S(2)}, u32[]{:S(2)}) %collective-permute-start.1) | collective-permute-done | bytes 49184 | tf_op jit(solution)/shard_map/ppermute | solution.py:467
  50.5 0.2 broadcast_in_dim.2
  50.6 18.9 %all_to_all.18 = f32[32,96,128]{2,1,0:T(8,128)S(1)} all-to-all(f32[32,96,128]{2,1,0:T(8,128)S(1)} %broadcast_in_dim.2), channel_id=1, replica_groups=mesh['zq'=2,'zp'=2,'x'=4,'y'=4,'zh'=2,'c'=2] {'zp','x','y'}, dimensions={0} | all-to-all | bytes 3145728 | tf_op jit(solution)/shard_map/all_to_all | solution.py:455
  69.5 9.5 %collective-permute-start.4 = (f32[3072,128]{1,0:T(8,128)S(1)}, f32[3072,128]{1,0:T(8,128)S(1)}, u32[]{:S(2)}, u32[]{:S(2)}) collective-permute-start(f32[3072,128]{1,0:T(8,128)S(1)} %bitcast.9), channel_id=1, source_target_pairs={{0,1},{1,0},{2,3},{3,2},{4,5},{5,4},{6,7},{7,6},{8,9},{9,8},{10,11... | collective-permute-start | bytes 4718600 | tf_op jit(solution)/shard_map/ppermute | solution.py:442
  79.0 1.7 %place.2 = (f32[512,512]{1,0:T(8,128)}, f32[512,512]{1,0:T(8,128)}, f32[500,512]{1,0:T(8,128)}, f32[1,500]{1,0:T(1,128)S(1)}, f32[1,1]{1,0:T(1,128)}) custom-call(f32[3072,128]{1,0:T(8,128)S(1)} %bitcast.10), custom_call_target="tpu_custom_call" | custom-call | flops 16777216 | bytes 3145728 | tf_op jit(solution)/shard_map/place/pallas_call | solution.py:403
  80.7 1.3 %collective-permute-done.4.refs_0_ = f32[3072,128]{1,0:T(8,128)S(1)} collective-permute-done((f32[3072,128]{1,0:T(8,128)S(1)}, f32[3072,128]{1,0:T(8,128)S(1)}, u32[]{:S(2)}, u32[]{:S(2)}) %collective-permute-start.4) | collective-permute-done | bytes 1572896 | tf_op jit(solution)/shard_map/ppermute | solution.py:442
  82.0 1.8 %place.3 = (f32[512,512]{1,0:T(8,128)}, f32[512,512]{1,0:T(8,128)}, f32[500,512]{1,0:T(8,128)}, f32[1,500]{1,0:T(1,128)}, f32[1,1]{1,0:T(1,128)}) custom-call(f32[3072,128]{1,0:T(8,128)S(1)} %collective-permute-done.4.refs_0_, f32[512,512]{1,0:T(8,128)} %get-tuple-element.18.refs_1_, ...), custom_call_target="tpu_custom_call", output_to_operand_aliasing={{0}: (1, {}), {1}: (2, {}), {2}: (3, {})} | custom-call | flops 16777216 | bytes 3145728 | tf_op jit(solution)/shard_map/place/pallas_call | solution.py:403
  (1 shorter events, 0.0 us)
Async XLA Ops:
  8.1 6.3 %collective-permute-start = (f32[3072,128]{1,0:T(8,128)S(1)}, f32[3072,128]{1,0:T(8,128)S(1)}, u32[]{:S(2)}, u32[]{:S(2)}) collective-permute-start(f32[3072,128]{1,0:T(8,128)S(1)} %get-tuple-element.17), channel_id=1, source_target_pairs={{0,1},{1,0},{2,3},{3,2},{4,5},{5,4},{6,7},{7,6},{8,9},{9,8},{10,11... | collective-permute-start | bytes 4718600 | tf_op jit(solution)/shard_map/ppermute | solution.py:442
  38.4 8.4 %collective-permute-start.3 = (f32[96,128]{1,0:T(8,128)S(1)}, f32[96,128]{1,0:T(8,128)S(1)}, u32[]{:S(2)}, u32[]{:S(2)}) collective-permute-start(f32[96,128]{1,0:T(8,128)S(1)} %reduce_sum.9), channel_id=1, source_target_pairs={{0,130},{128,0},{2,128},{130,2},{1,131},{129,1},{3,129},{131,3},{4... | collective-permute-start | bytes 147464 | tf_op jit(solution)/shard_map/ppermute | solution.py:467
  43.6 5.0 %collective-permute-start.2 = (f32[96,128]{1,0:T(8,128)S(1)}, f32[96,128]{1,0:T(8,128)S(1)}, u32[]{:S(2)}, u32[]{:S(2)}) collective-permute-start(f32[96,128]{1,0:T(8,128)S(1)} %reduce_sum.9), channel_id=1, source_target_pairs={{0,128},{128,2},{2,130},{130,0},{1,129},{129,3},{3,131},{131,1},{4... | collective-permute-start | bytes 147464 | tf_op jit(solution)/shard_map/ppermute | solution.py:467
  43.6 6.8 %collective-permute-start.1 = (f32[96,128]{1,0:T(8,128)S(1)}, f32[96,128]{1,0:T(8,128)S(1)}, u32[]{:S(2)}, u32[]{:S(2)}) collective-permute-start(f32[96,128]{1,0:T(8,128)S(1)} %reduce_sum.9), channel_id=1, source_target_pairs={{0,2},{128,130},{2,0},{130,128},{1,3},{129,131},{3,1},{131,129},{4... | collective-permute-start | bytes 147464 | tf_op jit(solution)/shard_map/ppermute | solution.py:467
  69.5 12.5 %collective-permute-start.4 = (f32[3072,128]{1,0:T(8,128)S(1)}, f32[3072,128]{1,0:T(8,128)S(1)}, u32[]{:S(2)}, u32[]{:S(2)}) collective-permute-start(f32[3072,128]{1,0:T(8,128)S(1)} %bitcast.9), channel_id=1, source_target_pairs={{0,1},{1,0},{2,3},{3,2},{4,5},{5,4},{6,7},{7,6},{8,9},{9,8},{10,11... | collective-permute-start | bytes 4718600 | tf_op jit(solution)/shard_map/ppermute | solution.py:442
